TPU v7x, 32 devices: a whole 2x2x4 slice. The times are simulated.
32 devices in a mesh: groups: 2 (over y), expert: 16 (over z, x, core), tensor: 1.
Axes of the slice: x: 2, y: 2, z: 4, core: 2. Of those that a mesh axis runs over, the one named last changes fastest.
Arguments:
- tokens: bfloat16 [64, 4096], P(('groups', 'expert')), parts along dimension 0, may hold values from -6 to 6
- expert_ids: int32 [64, 2], P(('groups', 'expert')), parts along dimension 0, may hold values from 0 to 3, all different within a row; in each aligned block of 2 rows (0 to 1, 2 to 3, ...) at most 2 rows name the same one
- gate_weights: float32 [64, 2], P(('groups', 'expert')), parts along dimension 0, may hold values from 0.2 to 1
- doc_ids: int32 [64], P(('groups', 'expert')), parts along dimension 0, may hold values from 0 to 3, never falling along the last dimension, each value on 1 to 16 neighbouring positions
- w_gate: bfloat16 [4096, 2048], P(None, ('expert', 'tensor')), may hold values from -0.09375 to 0.09375
- w_up: bfloat16 [4096, 2048], P(None, ('expert', 'tensor')), may hold values from -0.09375 to 0.09375
- w_down: bfloat16 [2048, 4096], P(('expert', 'tensor')), may hold values from -0.25 to 0.25
- w_score: float32 [4096], P('tensor'), may hold values from -0.375 to 0.375
Outputs:
- mixed: bfloat16 [64, 4096], P(('groups', 'expert'), 'tensor'), parts along dimension 0
- scores: float32 [8], P('groups'), parts along dimension 0
There are 2 independent parts, one for each index of `groups`. A program takes and returns all parts, laid end to end along the dimension named above; an argument that names none is the same for every part. Nothing has to cross between parts.
Inputs may be any that keep to these rules, and one draw needn't show every extreme that they name: `expert_ids`: each row names two different experts. Among the rows of one device no expert is named more than 2 times, and in some devices' rows some expert exactly 2 times. `doc_ids`: document ids never fall along the tokens; every document holds 1 to 16 tokens, one exactly 16.
All inputs are finite; a program needn't handle non-finite values.
Results may differ from a plain program's by a relative error of at most 0.0057.
Values may be sent and summed in bfloat16 or wider, within the bound.
No kernel may reach another device: no remote copies, remote signals or barrier semaphores. Data moves between devices by JAX's collectives and lax.ppermute only.
A program may use at most 64 MiB of HBM per device.

v0:
```python
import jax
import jax.numpy as jnp
from jax import lax
from jax.sharding import PartitionSpec as P

EXP_FLIGHT = 4
CAP = 2


def expert_block(rows, w_gate, w_up, w_down):
    shape_in = rows.shape
    flat = rows.reshape(-1, shape_in[-1])
    gate_part = jnp.dot(flat, w_gate, preferred_element_type=jnp.float32)
    up_part = jnp.dot(flat, w_up, preferred_element_type=jnp.float32)
    hidden = (jax.nn.silu(gate_part) * up_part).astype(jnp.bfloat16)
    partial_value = jnp.dot(hidden, w_down, preferred_element_type=jnp.float32).astype(jnp.bfloat16)
    partial_value = partial_value.reshape(shape_in)
    return lax.all_to_all(partial_value, "expert", split_axis=0, concat_axis=0, tiled=True)


def local(tokens, expert_ids, gate_weights, doc_ids, w_gate, w_up, w_down, w_score):
    expert_count = lax.axis_size("expert")
    tok_rows = tokens.shape[0]
    width = tokens.shape[1]
    spread = expert_count // EXP_FLIGHT
    slots_all = EXP_FLIGHT * CAP
    flat_ids = expert_ids.reshape(-1)
    picks = (flat_ids[:, None] == jnp.arange(EXP_FLIGHT, dtype=jnp.int32)[None, :]).astype(
        jnp.int32
    )
    earlier = jnp.cumsum(picks, axis=0) - picks
    slot_of = jnp.sum(earlier * picks, axis=1)
    target = flat_ids * CAP + slot_of
    places = jnp.arange(slots_all, dtype=jnp.int32)[:, None] == target[None, :]
    doubled = jnp.repeat(tokens, 2, axis=0)
    packed = jnp.dot(
        places.astype(jnp.bfloat16), doubled, preferred_element_type=jnp.float32
    ).astype(jnp.bfloat16)
    packed = packed.reshape(EXP_FLIGHT, 1, CAP, width)
    outgoing = jnp.broadcast_to(packed, (EXP_FLIGHT, spread, CAP, width)).reshape(
        expert_count, CAP, width
    )
    returned = expert_block(
        lax.all_to_all(outgoing, "expert", split_axis=0, concat_axis=0, tiled=True),
        w_gate,
        w_up,
        w_down,
    )
    summed = jnp.sum(returned.reshape(EXP_FLIGHT, spread, CAP, width), axis=1, dtype=jnp.float32)
    summed = summed.reshape(slots_all, width)
    weights_flat = gate_weights.reshape(-1)
    assign = jnp.where(places.T, weights_flat[:, None], jnp.float32(0.0))
    per_assign = jnp.dot(assign, summed, precision=lax.Precision.HIGHEST)
    mixed_part = jnp.sum(per_assign.reshape(tok_rows, 2, width), axis=1)
    mixed_wide = lax.psum_scatter(mixed_part, "tensor", scatter_dimension=1, tiled=True)
    mixed = mixed_wide.astype(jnp.bfloat16)
    projected = jnp.dot(mixed.astype(jnp.float32), w_score, precision=lax.Precision.HIGHEST)
    doc_total = tok_rows * expert_count // 8
    docs_hit = (doc_ids[:, None] == jnp.arange(doc_total, dtype=jnp.int32)[None, :]).astype(
        jnp.float32
    )
    doc_sums = jnp.dot(projected, docs_hit, precision=lax.Precision.HIGHEST)
    doc_counts = jnp.where(
        lax.axis_index("tensor") == 0, jnp.sum(docs_hit, axis=0), jnp.float32(0.0)
    )
    totals, counts = lax.psum((doc_sums, doc_counts), ("expert", "tensor"))
    scores = jax.nn.sigmoid(totals / counts)
    return (mixed, scores)


def solution(mesh):
    in_specs = (
        P(("groups", "expert"), None),
        P(("groups", "expert"), None),
        P(("groups", "expert"), None),
        P(("groups", "expert")),
        P(None, ("expert", "tensor")),
        P(None, ("expert", "tensor")),
        P(("expert", "tensor"), None),
        P("tensor"),
    )
    out_specs = (P(("groups", "expert"), "tensor"), P("groups"))
    return jax.shard_map(local, mesh=mesh, in_specs=in_specs, out_specs=out_specs, check_vma=False)
```

profile of v0, /device:TPU:0, one launch (start us, length us, event | category | flops | bytes accessed | tf_op | source)
XLA Modules:
  0.0 70.3 jit_solution(13723312300678550193)
XLA Ops:
  0.6 0.0 copy-start
  0.6 0.0 copy-start.1
  0.7 0.9 %eq.64 = s32[4]{0:T(128)S(1)} reshape(s32[2,2]{1,0:T(2,128)} %param.9) | data formatting | bytes 32 | tf_op jit(solution)/shard_map/eq | solution.py:28
  1.6 0.1 fusion.10
  1.7 0.2 select_reduce_fusion
  1.9 0.7 %broadcast_in_dim.31 = bf16[2,2,4096]{2,1,0:T(2,128)(2,1)S(1)} broadcast(bf16[2,4096]{1,0:T(2,128)(2,1)} %param.8), dimensions={0,2} | broadcast | bytes 49152 | tf_op jit(solution)/shard_map/broadcast_in_dim | solution.py:35
  2.6 0.1 convolution_convert_fusion.1
  2.8 0.1 broadcast_in_dim.32
  2.8 0.2 broadcast_in_dim.33
  3.1 17.3 %all_to_all.10 = bf16[16,2,4096]{2,1,0:T(2,128)(2,1)} all-to-all(bf16[16,2,4096]{2,1,0:T(2,128)(2,1)S(1)} %bitcast.23), channel_id=1, replica_groups=mesh['groups'=2,'expert'=16,'tensor'=1] {'expert'}, dimensions={0} | all-to-all | bytes 524288 | tf_op jit(solution)/shard_map/all_to_all | solution.py:44
  20.4 0.0 copy-start.2
  20.4 1.1 %reshape.70 = bf16[32,4096]{1,0:T(8,128)(2,1)S(1)} reshape(bf16[16,2,4096]{2,1,0:T(2,128)(2,1)} %all_to_all.10) | data formatting | bytes 524288 | tf_op jit(solution)/shard_map/reshape | solution.py:12
  21.5 0.0 copy-done.1
  21.5 0.3 fusion.18
  21.8 0.0 copy-done
  21.8 0.0 copy-done.2
  21.8 0.5 convolution_convert_fusion
  22.4 0.9 %reshape.71 = bf16[16,2,4096]{2,1,0:T(2,128)(2,1)} reshape(bf16[32,4096]{1,0:T(8,128)(2,1)S(1)} %convolution_convert_fusion) | data formatting | bytes 524288 | tf_op jit(solution)/shard_map/reshape | solution.py:17
  23.2 3.5 %all-to-all-start.1 = ((bf16[16,2,4096]{2,1,0:T(2,128)(2,1)}), bf16[16,2,4096]{2,1,0:T(2,128)(2,1)S(1)}, u32[]{:S(2)}, u32[]{:S(2)}) async-start(bf16[16,2,4096]{2,1,0:T(2,128)(2,1)} %reshape.71), calls=%async_computation.1 | async-start | bytes 524288 | tf_op jit(solution)/shard_map/all_to_all | solution.py:18
  26.8 0.0 copy-start.7
  26.8 0.1 reduce_sum.39
  26.9 0.6 copy-done.7
  27.4 0.0 copy-start.5
  27.4 0.1 convert_reduce_fusion.1
  27.5 0.6 copy-done.5
  28.1 8.6 %all-to-all-done.1 = bf16[16,2,4096]{2,1,0:T(2,128)(2,1)S(1)} async-done(((bf16[16,2,4096]{2,1,0:T(2,128)(2,1)}), bf16[16,2,4096]{2,1,0:T(2,128)(2,1)S(1)}, u32[]{:S(2)}, u32[]{:S(2)}) %all-to-all-start.1) | async-done | bytes 262176 | tf_op jit(solution)/shard_map/all_to_all | solution.py:18
  36.8 0.3 convert_reduce_fusion
  37.0 0.0 copy-start.4
  37.0 0.1 reshape.74
  37.1 0.6 copy-done.4
  37.7 0.0 copy-start.6
  37.7 0.4 convolution_reduce_fusion
  38.2 0.0 copy-start.3
  38.2 0.3 copy-done.6
  38.4 0.2 convolution_bitcast_fusion.1
  38.6 0.1 copy-done.3
  38.8 0.2 convolution_bitcast_fusion
  39.0 30.8 %all-reduce = (f32[4]{0:T(128)S(1)}, f32[4]{0:T(128)S(1)}) all-reduce(f32[4]{0:T(128)S(1)} %convolution_bitcast_fusion, f32[4]{0:T(128)S(1)} %convert_reduce_fusion.1), channel_id=1, replica_groups=mesh['groups'=2,'expert'=16,'tensor'=1] {'expert','tensor'}, use_global_device_ids=true, to_apply=%region_4.5 | all-reduce | flops 8 | bytes 64 | tf_op jit(solution)/shard_map/psum | solution.py:66
  69.7 0.5 add_divide_fusion
  (4 shorter events, 0.1 us)
Async XLA Ops:
  0.6 21.2 %copy-start = (bf16[128,4096]{1,0:T(8,128)(2,1)S(1)}, bf16[128,4096]{1,0:T(8,128)(2,1)}, u32[]{:S(2)}) copy-start(bf16[128,4096]{1,0:T(8,128)(2,1)} %param.14) | copy-start | bytes 3145732
  0.6 20.9 %copy-start.1 = (bf16[4096,128]{1,0:T(8,128)(2,1)S(1)}, bf16[4096,128]{1,0:T(8,128)(2,1)}, u32[]{:S(2)}) copy-start(bf16[4096,128]{1,0:T(8,128)(2,1)} %param.12) | copy-start | bytes 3145732
  20.4 1.5 %copy-start.2 = (bf16[4096,128]{1,0:T(8,128)(2,1)S(1)}, bf16[4096,128]{1,0:T(8,128)(2,1)}, u32[]{:S(2)}) copy-start(bf16[4096,128]{1,0:T(8,128)(2,1)} %param.13) | copy-start | bytes 3145732
  23.2 13.5 %all-to-all-start.1 = ((bf16[16,2,4096]{2,1,0:T(2,128)(2,1)}), bf16[16,2,4096]{2,1,0:T(2,128)(2,1)S(1)}, u32[]{:S(2)}, u32[]{:S(2)}) async-start(bf16[16,2,4096]{2,1,0:T(2,128)(2,1)} %reshape.71), calls=%async_computation.1 | async-start | bytes 524288 | tf_op jit(solution)/shard_map/all_to_all | solution.py:18
  26.8 0.7 copy-start.7
  27.4 0.7 copy-start.5
  37.0 0.7 copy-start.4
  37.7 0.7 %copy-start.6 = (f32[4096]{0:T(1024)S(1)}, f32[4096]{0:T(1024)}, u32[]{:S(2)}) copy-start(f32[4096]{0:T(1024)} %param.15) | copy-start | bytes 49156
  38.2 0.6 copy-start.3
where the time goes:
time: 70.8 us; the launch traced here: 70.3 us
  blocking collectives  48.1 us (68%)
  waiting for transfers between devices  8.64 us (12%)
  local copies, waits for them, and re-layouts  6.27 us (9%)
  starting transfers between devices  3.53 us (5%)
  matrix products  1.79 us (3%)
  other arithmetic  1.19 us (2%)
  between operations  0.77 us (1%)
    psum x1, blocking collectives, local(): totals, counts = lax.psum((doc_sums, doc_counts), ('expert', 'tensor'))  30.8 us
    all_to_all x1, blocking collectives, local(): lax.all_to_all(outgoing, 'expert', split_axis=0, concat_axis=0, tiled=True)  17.3 us
    all_to_all x1, waiting for transfers between devices, expert_block(): lax.all_to_all(partial_value, 'expert', split_axis=0, concat_axis=0, tile...  8.64 us
    all_to_all x1, starting transfers between devices, expert_block(): lax.all_to_all(partial_value, 'expert', split_axis=0, concat_axis=0, tile...  3.53 us
    unnamed x16, local copies, waits for them, and re-layouts  2.15 us
  transfers between devices with their start and end apart: 1, of which 1 were waited for; matrix products, arithmetic and copies ran while one was open for 0% of the time, Pallas kernels for 0%

commit v1 on v0

v1 whole, which is shorter than its diff:
```python
import jax
import jax.numpy as jnp
from jax import lax
from jax.sharding import PartitionSpec as P

EXP_FLIGHT = 4
LANES = 128
PIECES = 3


def split_wide(value):
    pieces = []
    rest = value
    for _ in range(PIECES):
        piece = lax.reduce_precision(rest, 8, 7)
        pieces.append(piece)
        rest = rest - piece
    return pieces


def side_lanes(columns, rows):
    lane = lax.broadcasted_iota(jnp.int32, (rows, LANES), 1)
    out = jnp.zeros((rows, LANES), jnp.float32)
    for at, column in enumerate(columns):
        out = jnp.where(lane == at, column, out)
    return out.astype(jnp.bfloat16)


def local(tokens, expert_ids, gate_weights, doc_ids, w_gate, w_up, w_down, w_score):
    members = lax.axis_size("expert")
    parts = lax.axis_size("tensor")
    tok_rows, width = tokens.shape
    rows = members * tok_rows
    spread = members // EXP_FLIGHT
    doc_total = rows // 8
    own_expert = lax.axis_index("expert") // spread

    columns = []
    for expert in range(EXP_FLIGHT):
        weight = jnp.sum(
            jnp.where(expert_ids == expert, gate_weights, jnp.float32(0.0)), axis=1, keepdims=True
        )
        columns += split_wide(weight)
    columns.append(doc_ids[:, None].astype(jnp.float32))
    outgoing = jnp.concatenate([tokens, side_lanes(columns, tok_rows)], axis=1)
    outgoing = jnp.broadcast_to(outgoing[None], (members, tok_rows, width + LANES))
    gathered = lax.all_to_all(outgoing, "expert", split_axis=0, concat_axis=0, tiled=True)
    gathered = gathered.reshape(rows, width + LANES)
    flat = gathered[:, :width]
    side = gathered[:, width:].astype(jnp.float32)

    gate_part = jnp.dot(flat, w_gate, preferred_element_type=jnp.float32)
    up_part = jnp.dot(flat, w_up, preferred_element_type=jnp.float32)
    hidden = (jax.nn.silu(gate_part) * up_part).astype(jnp.bfloat16)
    partial_value = jnp.dot(hidden, w_down, preferred_element_type=jnp.float32)

    lane = lax.broadcasted_iota(jnp.int32, (rows, LANES), 1)
    mine = (lane >= own_expert * PIECES) & (lane < (own_expert + 1) * PIECES)
    weight = jnp.sum(jnp.where(mine, side, jnp.float32(0.0)), axis=1, keepdims=True)
    docs = side[:, EXP_FLIGHT * PIECES].astype(jnp.int32)
    weighted = (partial_value * weight).astype(jnp.bfloat16)

    score_full = lax.all_gather(w_score, "tensor", axis=0, tiled=True) if parts > 1 else w_score
    projected = jnp.sum(weighted.astype(jnp.float32) * score_full[None, :], axis=1)
    hits = (docs[:, None] == jnp.arange(doc_total, dtype=jnp.int32)[None, :]).astype(jnp.float32)
    counts = jnp.sum(hits, axis=0)
    doc_part = jnp.sum(hits * projected[:, None], axis=0)

    pieces = jnp.concatenate(split_wide(doc_part))
    side_out = jnp.zeros((LANES,), jnp.float32).at[: PIECES * doc_total].set(pieces)
    side_out = jnp.broadcast_to(side_out.astype(jnp.bfloat16), (rows, LANES))
    leaving = jnp.concatenate([weighted, side_out], axis=1).reshape(
        members, tok_rows, width + LANES
    )
    returned = lax.all_to_all(leaving, "expert", split_axis=0, concat_axis=0, tiled=True)
    summed = jnp.sum(returned.astype(jnp.float32), axis=0)
    mixed = lax.psum_scatter(summed[:, :width], "tensor", scatter_dimension=1, tiled=True)
    mixed = mixed.astype(jnp.bfloat16)
    totals = summed[0, width : width + PIECES * doc_total].reshape(PIECES, doc_total).sum(axis=0)
    totals = lax.psum(totals, "tensor")
    scores = jax.nn.sigmoid(totals / counts)
    return (mixed, scores)


def solution(mesh):
    in_specs = (
        P(("groups", "expert"), None),
        P(("groups", "expert"), None),
        P(("groups", "expert"), None),
        P(("groups", "expert")),
        P(None, ("expert", "tensor")),
        P(None, ("expert", "tensor")),
        P(("expert", "tensor"), None),
        P("tensor"),
    )
    out_specs = (P(("groups", "expert"), "tensor"), P("groups"))
    return jax.shard_map(local, mesh=mesh, in_specs=in_specs, out_specs=out_specs, check_vma=False)
```

time: 70.8 us -> 39.7 us (0.56)
  blocking collectives: 48.1 us -> 12.9 us
  starting transfers between devices: 3.53 us -> 7.39 us
  local copies, waits for them, and re-layouts: 6.27 us -> 4.19 us
  waiting for transfers between devices: 8.64 us -> 10.1 us
    psum x1 -> x0, blocking collectives: 30.8 us -> none  [local(): totals, counts = lax.psum((doc_sums, doc_counts), ('expert', 'tensor'))]
    all_to_all x1, blocking collectives: 17.3 us -> 12.9 us  [local(): lax.all_to_all(leaving, 'expert', split_axis=0, concat_axis=0, tiled=True)]
    all_to_all x1, starting transfers between devices: 3.53 us -> 7.39 us  [local(): lax.all_to_all(outgoing, 'expert', split_axis=0, concat_axis=0, tiled=True)]
    reshape x4 -> x2, local copies, waits for them, and re-layouts: 2.13 us -> 0.21 us  [the longest x1 0.1 us: local(): jnp.concatenate([weighted, side_out], axis=1)]
    all_to_all x1, waiting for transfers between devices: 8.64 us -> 10.1 us  [local(): lax.all_to_all(outgoing, 'expert', split_axis=0, concat_axis=0, tiled=True)]
    eq x1 -> x0, local copies, waits for them, and re-layouts: 0.91 us -> none  [local(): flat_ids[:, None] == jnp.arange(EXP_FLIGHT, dtype=jnp.int32)[None, :]]
    dot_general x6 -> x2, matrix products: 1.79 us -> 2.17 us  [the longest x1 1.5 us: local(): gate_part = jnp.dot(flat, w_gate, preferred_element_type=jnp.float32)]
    unnamed x16 -> x14, local copies, waits for them, and re-layouts: 2.15 us -> 2.41 us
where the time goes in v1:
time: 39.7 us; the launch traced here: 39.3 us
  blocking collectives  12.9 us (32%)
  waiting for transfers between devices  10.1 us (25%)
  starting transfers between devices  7.39 us (19%)
  local copies, waits for them, and re-layouts  4.19 us (11%)
  matrix products  2.17 us (5%)
  other arithmetic  1.7 us (4%)
  between operations  0.84 us (2%)
    all_to_all x1, blocking collectives, local(): lax.all_to_all(leaving, 'expert', split_axis=0, concat_axis=0, tiled=True)  12.9 us
    all_to_all x1, waiting for transfers between devices, local(): lax.all_to_all(outgoing, 'expert', split_axis=0, concat_axis=0, tiled=True)  10.1 us
    all_to_all x1, starting transfers between devices, local(): lax.all_to_all(outgoing, 'expert', split_axis=0, concat_axis=0, tiled=True)  7.39 us
    unnamed x14, local copies, waits for them, and re-layouts  2.41 us
    dot_general x1, matrix products, local(): gate_part = jnp.dot(flat, w_gate, preferred_element_type=jnp.float32)  1.5 us
    broadcast_in_dim x1, local copies, waits for them, and re-layouts, local(): jnp.broadcast_to(outgoing[None], (members, tok_rows, width + LANES))  0.85 us
  transfers between devices with their start and end apart: 1, of which 1 were waited for; matrix products, arithmetic and copies ran while one was open for 0% of the time, Pallas kernels for 0%

profile of v1, /device:TPU:0, one launch (start us, length us, event | category | flops | bytes accessed | tf_op | source)
XLA Modules:
  0.0 39.3 jit_solution(14353964959674738390)
XLA Ops:
  0.6 0.0 copy-start
  0.7 0.0 copy-start.6
  0.7 0.0 copy-start.5
  0.8 0.7 %copy-done.6 = s32[2]{0:T(128)S(1)} copy-done((s32[2]{0:T(128)S(1)}, s32[2]{0:T(128)}, u32[]{:S(2)}) %copy-start.6) | copy-done | bytes 32
  1.4 0.0 copy-start.4
  1.5 0.0 copy-done.5
  1.5 0.6 %copy-done.4 = f32[2,2]{1,0:T(2,128)S(1)} copy-done((f32[2,2]{1,0:T(2,128)S(1)}, f32[2,2]{1,0:T(2,128)}, u32[]{:S(2)}) %copy-start.4) | copy-done | bytes 40
  2.1 0.1 fusion.13
  2.3 0.0 copy-start.3
  2.3 0.1 select_convert_fusion
  2.4 0.6 %copy-done.3 = bf16[2,4096]{1,0:T(2,128)(2,1)S(1)} copy-done((bf16[2,4096]{1,0:T(2,128)(2,1)S(1)}, bf16[2,4096]{1,0:T(2,128)(2,1)}, u32[]{:S(2)}) %copy-start.3) | copy-done | bytes 16408
  3.0 0.8 %broadcast_in_dim.117 = bf16[16,2,4224]{2,1,0:T(2,128)(2,1)} broadcast(bf16[2,4224]{1,0:T(2,128)(2,1)S(1)} %pad_maximum_fusion.1), dimensions={1,2} | broadcast | bytes 287232 | tf_op jit(solution)/shard_map/broadcast_in_dim | solution.py:46
  3.9 7.4 %all-to-all-start = ((bf16[16,2,4224]{2,1,0:T(2,128)(2,1)}), bf16[16,2,4224]{2,1,0:T(2,128)(2,1)S(1)}, u32[]{:S(2)}, u32[]{:S(2)}) async-start(bf16[16,2,4224]{2,1,0:T(2,128)(2,1)} %broadcast_in_dim.117), calls=%async_computation | async-start | bytes 540672 | tf_op jit(solution)/shard_map/all_to_all | solution.py:47
  11.3 0.0 copy-start.1
  11.3 10.1 %all-to-all-done = bf16[16,2,4224]{2,1,0:T(2,128)(2,1)S(1)} async-done(((bf16[16,2,4224]{2,1,0:T(2,128)(2,1)}), bf16[16,2,4224]{2,1,0:T(2,128)(2,1)S(1)}, u32[]{:S(2)}, u32[]{:S(2)}) %all-to-all-start) | async-done | bytes 270368 | tf_op jit(solution)/shard_map/all_to_all | solution.py:47
  21.4 0.1 reshape.102
  21.6 1.5 %fusion.4 = f32[32,128]{1,0:T(8,128)S(1)} fusion(bf16[4096,128]{1,0:T(8,128)(2,1)} %param.14, bf16[32,4224]{1,0:T(8,128)(2,1)S(1)} %reshape.102), kind=kOutput, calls=%fused_computation.8 | convolution fusion | flops 33554432 | bytes 1327104 | tf_op jit(solution)/shard_map/dot_general | solution.py:52
  23.1 0.0 copy-start.2
  23.1 0.1 select_reduce_fusion
  23.2 0.2 fusion.6
  23.4 0.0 copy-done
  23.4 0.0 copy-done.1
  23.4 0.4 %copy-done.2 = f32[4096]{0:T(1024)S(1)} copy-done((f32[4096]{0:T(1024)S(1)}, f32[4096]{0:T(1024)}, u32[]{:S(2)}) %copy-start.2) | copy-done | bytes 16408
  23.8 0.7 %multiply_reduce_fusion = (f32[32]{0:T(128)S(1)}, bf16[32,4096]{1,0:T(8,128)(2,1)S(1)}) fusion(f32[4096]{0:T(1024)S(1)} %copy-done.2, f32[32]{0:T(128)S(1)} %select_reduce_fusion, bf16[128,4096]{1,0:T(8,128)(2,1)S(1)} %copy-done, bf16[4096,128]{1,0:T(8,128)(2,1)S(1)} %copy-done.1, bf16[32,4224]{1,0:T(8,128)(2,1)S(1)} %reshape.102, f32[32,128]{1,0:T(8,128)S(1)} %fusion.4), kind=kOutput, calls=%fused_computation.5 | convolution fusion | flops 67788768 | bytes 2654848 | tf_op jit(solution)/shard_map/dot_general | solution.py:55
  24.5 0.2 convert_reduce_fusion.1
  24.6 0.1 select_maximum_fusion
  24.7 0.1 pad_maximum_fusion
  24.8 0.1 reshape.103
  24.9 12.9 %all_to_all.10 = bf16[16,2,4224]{2,1,0:T(2,128)(2,1)S(1)} all-to-all(bf16[16,2,4224]{2,1,0:T(2,128)(2,1)S(1)} %reshape.103), channel_id=1, replica_groups=mesh['groups'=2,'expert'=16,'tensor'=1] {'expert'}, dimensions={0} | all-to-all | bytes 540672 | tf_op jit(solution)/shard_map/all_to_all | solution.py:75
  37.7 0.2 convert_reduce_fusion
  38.0 0.6 %slice.50 = bf16[2,4096]{1,0:T(2,128)(2,1)} slice(f32[2,4224]{1,0:T(2,128)S(1)} %convert_reduce_fusion), slice={[0:2], [0:4096]} | slice | bytes 32768 | tf_op jit(solution)/shard_map/slice | solution.py:77
  38.6 0.1 reshape_squeeze.3
  38.7 0.5 %add_divide_fusion = f32[4]{0:T(128)} fusion(f32[4]{0:T(128)S(1)} %reduce_sum.98, f32[4]{0:T(128)S(1)} %get-tuple-element.18), kind=kLoop, calls=%fused_computation.45 | loop fusion | flops 16 | bytes 48 | tf_op jit(solution)/shard_map/div | solution.py:81
  (17 shorter events, 0.2 us)
Async XLA Ops:
  0.6 22.7 %copy-start = (bf16[128,4096]{1,0:T(8,128)(2,1)S(1)}, bf16[128,4096]{1,0:T(8,128)(2,1)}, u32[]{:S(2)}) copy-start(bf16[128,4096]{1,0:T(8,128)(2,1)} %param.16) | copy-start | bytes 3145732
  0.7 0.7 %copy-start.6 = (s32[2]{0:T(128)S(1)}, s32[2]{0:T(128)}, u32[]{:S(2)}) copy-start(s32[2]{0:T(128)} %param.13) | copy-start | bytes 28
  0.7 0.8 %copy-start.5 = (s32[2,2]{1,0:T(2,128)S(1)}, s32[2,2]{1,0:T(2,128)}, u32[]{:S(2)}) copy-start(s32[2,2]{1,0:T(2,128)} %param.11) | copy-start | bytes 52
  1.4 0.7 %copy-start.4 = (f32[2,2]{1,0:T(2,128)S(1)}, f32[2,2]{1,0:T(2,128)}, u32[]{:S(2)}) copy-start(f32[2,2]{1,0:T(2,128)} %param.12) | copy-start | bytes 52
  2.3 0.7 %copy-start.3 = (bf16[2,4096]{1,0:T(2,128)(2,1)S(1)}, bf16[2,4096]{1,0:T(2,128)(2,1)}, u32[]{:S(2)}) copy-start(bf16[2,4096]{1,0:T(2,128)(2,1)} %param.10) | copy-start | bytes 49156
  3.9 17.5 %all-to-all-start = ((bf16[16,2,4224]{2,1,0:T(2,128)(2,1)}), bf16[16,2,4224]{2,1,0:T(2,128)(2,1)S(1)}, u32[]{:S(2)}, u32[]{:S(2)}) async-start(bf16[16,2,4224]{2,1,0:T(2,128)(2,1)} %broadcast_in_dim.117), calls=%async_computation | async-start | bytes 540672 | tf_op jit(solution)/shard_map/all_to_all | solution.py:47
  11.3 12.1 %copy-start.1 = (bf16[4096,128]{1,0:T(8,128)(2,1)S(1)}, bf16[4096,128]{1,0:T(8,128)(2,1)}, u32[]{:S(2)}) copy-start(bf16[4096,128]{1,0:T(8,128)(2,1)} %param.15) | copy-start | bytes 3145732
  23.1 0.7 %copy-start.2 = (f32[4096]{0:T(1024)S(1)}, f32[4096]{0:T(1024)}, u32[]{:S(2)}) copy-start(f32[4096]{0:T(1024)} %param.17) | copy-start | bytes 49156

commit v2 on v1

v2 whole, which is shorter than its diff:
```python
import functools

import jax
import jax.numpy as jnp
from jax import lax
from jax.experimental import pallas as pl
from jax.experimental.pallas import tpu as pltpu
from jax.sharding import PartitionSpec as P

EXP_FLIGHT = 4
LANES = 128
VMEM_LIMIT = 24 * 1024 * 1024
LOAD_FLOPS = 10_000_000


def split_pair(value):
    high = value.astype(jnp.bfloat16).astype(jnp.float32)
    low = (value - high).astype(jnp.bfloat16).astype(jnp.float32)
    return high, low


def call(body, outs, args, in_spaces=None, out_spaces=None, cost=None, scratch=(), limit=VMEM_LIMIT):
    vmem = pltpu.MemorySpace.VMEM
    ins = in_spaces or [vmem] * len(args)
    spaces = out_spaces or [vmem] * len(outs)
    return pl.pallas_call(
        body,
        out_shape=tuple(outs),
        in_specs=[pl.BlockSpec(memory_space=s) for s in ins],
        out_specs=tuple(pl.BlockSpec(memory_space=s) for s in spaces),
        compiler_params=pltpu.CompilerParams(vmem_limit_bytes=limit),
        cost_estimate=cost,
        scratch_shapes=scratch,
    )(*args)


def in_hbm(*arrays):
    return tuple(pltpu.with_memory_space_constraint(a, pltpu.MemorySpace.HBM) for a in arrays)


def pack_body(tokens_ref, ids_ref, gates_ref, docs_ref, out_ref, ids, gates, docs, sems):
    blocks, rows, _ = out_ref.shape
    width = tokens_ref.shape[1]
    small = [
        pltpu.make_async_copy(ids_ref, ids, sems.at[0]),
        pltpu.make_async_copy(gates_ref, gates, sems.at[1]),
        pltpu.make_async_copy(docs_ref, docs, sems.at[2]),
    ]
    large = [
        pltpu.make_async_copy(tokens_ref, out_ref.at[b, :, pl.ds(0, width)], sems.at[3 + b])
        for b in range(blocks)
    ]
    for copy in small + large:
        copy.start()
    for copy in small:
        copy.wait()
    lane = lax.broadcasted_iota(jnp.int32, (rows, LANES), 1)
    row = lax.broadcasted_iota(jnp.int32, (rows, LANES), 0)
    weight = jnp.zeros((rows, LANES), jnp.float32)
    doc = jnp.zeros((rows, LANES), jnp.float32)
    for r in range(rows):
        for k in range(ids.shape[1]):
            named = ids[r, k]
            hit = (row == r) & ((lane == named) | (lane == named + EXP_FLIGHT))
            weight = jnp.where(hit, gates[r, k], weight)
        doc = jnp.where(row == r, docs[r].astype(jnp.float32), doc)
    high, low = split_pair(weight)
    side = jnp.where(lane < EXP_FLIGHT, high, low)
    side = jnp.where(lane == 2 * EXP_FLIGHT, doc, side).astype(jnp.bfloat16)
    for b in range(blocks):
        out_ref[b, :, width:] = side
    for copy in large:
        copy.wait()


def load_body(*refs):
    count = (len(refs) - 1) // 2
    sems = refs[-1]
    copies = [
        pltpu.make_async_copy(refs[i], refs[count + i], sems.at[i]) for i in range(count)
    ]
    for copy in copies:
        copy.start()
    for copy in copies:
        copy.wait()


def expert_rows(spread, block, w_gate_ref, w_up_ref, w_down_ref, w_score_ref):
    blocks, each, total = block.shape
    rows = blocks * each
    width = total - LANES
    flat = block.reshape(rows, total)
    held = flat[:, :width]
    side = flat[:, width:].astype(jnp.float32)
    gate = jnp.dot(held, w_gate_ref[...], preferred_element_type=jnp.float32)
    up = jnp.dot(held, w_up_ref[...], preferred_element_type=jnp.float32)
    hidden = (gate / (1.0 + jnp.exp(-gate)) * up).astype(jnp.bfloat16)
    part = jnp.dot(hidden, w_down_ref[...], preferred_element_type=jnp.float32)
    own = lax.axis_index("expert") // spread
    lane = lax.broadcasted_iota(jnp.int32, (rows, LANES), 1)
    mine = (lane == own) | (lane == own + EXP_FLIGHT)
    weight = jnp.sum(jnp.where(mine, side, 0.0), axis=1, keepdims=True)
    doc = jnp.sum(jnp.where(lane == 2 * EXP_FLIGHT, side, 0.0), axis=1, keepdims=True)
    part = part * weight
    projected = jnp.sum(part * w_score_ref[...], axis=1, keepdims=True)
    hits = doc == lane.astype(jnp.float32)
    sums = jnp.sum(jnp.where(hits, projected, 0.0), axis=0, keepdims=True)
    counts = jnp.sum(jnp.where(hits, 1.0, 0.0), axis=0, keepdims=True)
    return part, sums, counts


def side_rows(sums, rows):
    row = lax.broadcasted_iota(jnp.int32, (rows, LANES), 0)
    high, low = split_pair(sums)
    side = jnp.where(row == 0, high, jnp.where(row == 1, low, 0.0))
    return side.astype(jnp.bfloat16)


def first_body(spread, x_ref, w_gate_ref, w_up_ref, w_down_ref, w_score_ref, part_ref, stat_ref):
    part, sums, counts = expert_rows(
        spread, x_ref[...], w_gate_ref, w_up_ref, w_down_ref, w_score_ref
    )
    part_ref[...] = part
    stat_ref[0:1] = sums
    stat_ref[1:2] = counts


def second_body(
    spread, x_ref, w_gate_ref, w_up_ref, w_down_ref, w_score_ref, before_ref, out_ref, stat_ref
):
    blocks, each, total = x_ref.shape
    width = total - LANES
    part, sums, counts = expert_rows(
        spread, x_ref[...], w_gate_ref, w_up_ref, w_down_ref, w_score_ref
    )
    sums = sums + before_ref[0:1]
    stat_ref[0:1] = sums
    stat_ref[1:2] = counts + before_ref[1:2]
    out_ref[:, :, :width] = part.astype(jnp.bfloat16).reshape(blocks, each, width)
    side = side_rows(sums, each)
    for b in range(blocks):
        out_ref[b, :, width:] = side


def add_body(part_ref, came_ref, stat_ref, out_ref):
    blocks, each, total = came_ref.shape
    width = total - LANES
    came = came_ref[...].reshape(blocks * each, total)
    added = part_ref[...] + came[:, :width].astype(jnp.float32)
    out_ref[:, :, :width] = added.astype(jnp.bfloat16).reshape(blocks, each, width)
    other = jnp.sum(came[:each, width:].astype(jnp.float32), axis=0, keepdims=True)
    side = side_rows(stat_ref[0:1] + other, each)
    for b in range(blocks):
        out_ref[b, :, width:] = side


def last_body(came_ref, stat_ref, mixed_ref, scores_ref):
    blocks, each, total = came_ref.shape
    width = total - LANES
    summed = came_ref[0].astype(jnp.float32)
    for b in range(1, blocks):
        summed = summed + came_ref[b].astype(jnp.float32)
    mixed_ref[...] = summed[:, :width].astype(jnp.bfloat16)
    totals = jnp.sum(summed[:, width:], axis=0, keepdims=True)
    ratio = totals / stat_ref[1:2]
    scores = 1.0 / (1.0 + jnp.exp(-ratio))
    lane = lax.broadcasted_iota(jnp.int32, (1, LANES), 1)
    for d in range(scores_ref.shape[0]):
        scores_ref[d] = jnp.sum(jnp.where(lane == d, scores, 0.0))


def local(tokens, expert_ids, gate_weights, doc_ids, w_gate, w_up, w_down, w_score):
    members = lax.axis_size("expert")
    parts = lax.axis_size("tensor")
    tok_rows, width = tokens.shape
    rows = members * tok_rows
    spread = members // EXP_FLIGHT
    doc_total = rows // 8
    half = members // 2
    total = width + LANES
    vmem, smem = pltpu.MemorySpace.VMEM, pltpu.MemorySpace.SMEM
    alike = [list(range(side, members, 2)) for side in range(2)]
    swap = [(i, i ^ 1) for i in range(members)]
    exchange = functools.partial(
        lax.all_to_all, axis_name="expert", split_axis=0, concat_axis=0, axis_index_groups=alike, tiled=True
    )
    packet = jax.ShapeDtypeStruct((half, tok_rows, total), jnp.bfloat16)
    stat = jax.ShapeDtypeStruct((2, LANES), jnp.float32)

    hbm = pltpu.MemorySpace.HBM

    (outgoing,) = call(
        pack_body,
        [packet],
        in_hbm(tokens, expert_ids, gate_weights, doc_ids),
        [hbm] * 4,
        scratch=(
            pltpu.SMEM(expert_ids.shape, jnp.int32),
            pltpu.SMEM(gate_weights.shape, jnp.float32),
            pltpu.SMEM(doc_ids.shape, jnp.int32),
            pltpu.SemaphoreType.DMA((3 + half,)),
        ),
    )
    score_full = lax.all_gather(w_score, "tensor", axis=0, tiled=True) if parts > 1 else w_score
    weights = (w_gate, w_up, w_down, score_full.reshape(1, -1))
    near = exchange(outgoing)
    size = sum(w.size * w.dtype.itemsize for w in weights)
    weights = call(
        load_body,
        [jax.ShapeDtypeStruct(w.shape, w.dtype) for w in weights],
        in_hbm(*weights),
        [hbm] * len(weights),
        cost=pl.CostEstimate(flops=LOAD_FLOPS, bytes_accessed=2 * size, transcendentals=0),
        scratch=(pltpu.SemaphoreType.DMA((len(weights),)),),
    )
    near, *weights = lax.optimization_barrier((near, *weights))
    far = lax.ppermute(near, "expert", swap)
    kept, stat_near = call(
        functools.partial(first_body, spread),
        [jax.ShapeDtypeStruct((rows // 2, width), jnp.float32), stat],
        (near, *weights),
    )
    leaving, stat_all = call(
        functools.partial(second_body, spread), [packet, stat], (far, *weights, stat_near)
    )
    came = lax.ppermute(leaving, "expert", swap)
    (sending,) = call(add_body, [packet], (kept, came, stat_all))
    returned = exchange(sending)
    if parts == 1:
        return call(
            last_body,
            [
                jax.ShapeDtypeStruct((tok_rows, width), jnp.bfloat16),
                jax.ShapeDtypeStruct((doc_total,), jnp.float32),
            ],
            (returned, stat_all),
            None,
            [vmem, smem],
        )
    summed = jnp.sum(returned.astype(jnp.float32), axis=0)
    mixed = lax.psum_scatter(summed[:, :width], "tensor", scatter_dimension=1, tiled=True)
    totals = lax.psum(jnp.sum(summed[:, width : width + doc_total], axis=0), "tensor")
    scores = jax.nn.sigmoid(totals / stat_all[1, :doc_total])
    return (mixed.astype(jnp.bfloat16), scores)


def solution(mesh):
    in_specs = (
        P(("groups", "expert"), None),
        P(("groups", "expert"), None),
        P(("groups", "expert"), None),
        P(("groups", "expert")),
        P(None, ("expert", "tensor")),
        P(None, ("expert", "tensor")),
        P(("expert", "tensor"), None),
        P("tensor"),
    )
    out_specs = (P(("groups", "expert"), "tensor"), P("groups"))
    return jax.shard_map(local, mesh=mesh, in_specs=in_specs, out_specs=out_specs, check_vma=False)
```

time: 39.7 us -> 31.7 us (0.80)
  Pallas kernels: 0 us -> 5.84 us
  local copies, waits for them, and re-layouts: 4.19 us -> 0 us
  blocking collectives: 12.9 us -> 10 us
  waiting for transfers between devices: 10.1 us -> 7.32 us
  matrix products: 2.17 us -> 0 us
  other arithmetic: 1.7 us -> 0 us
    pallas_call x0 -> x6, Pallas kernels: none -> 5.84 us  [call(): pl.pallas_call(body, out_shape=tuple(outs), in_specs=[pl.BlockSpec(memory...]
    all_to_all x1, waiting for transfers between devices: 10.1 us -> 5.47 us  [local(): near = exchange(outgoing)]
    all_to_all x1, blocking collectives: 12.9 us -> 10 us  [local(): returned = exchange(sending)]
    unnamed x14 -> x0, local copies, waits for them, and re-layouts: 2.41 us -> none
    dot_general x2 -> x0, matrix products: 2.17 us -> none  [the longest x1 1.5 us: local(): gate_part = jnp.dot(flat, w_gate, preferred_element_type=jnp.float32)]
    ppermute x0 -> x2, waiting for transfers between devices: none -> 1.85 us  [the longest x1 1.21 us: local(): came = lax.ppermute(leaving, 'expert', swap)]
    broadcast_in_dim x1 -> x0, local copies, waits for them, and re-layouts: 0.85 us -> none  [local(): jnp.broadcast_to(outgoing[None], (members, tok_rows, width + LANES))]
    reduce_sum x5 -> x0, other arithmetic: 0.65 us -> none  [the longest x1 0.22 us: local(): summed = jnp.sum(returned.astype(jnp.float32), axis=0)]
  transfers between devices with their start and end apart: 1 -> 3, of which waited for: 1 -> 3; matrix products, arithmetic and copies ran while one was open for 0% -> 0% of each run, Pallas kernels for 0% -> 8%
where the time goes in v2:
time: 31.7 us; the launch traced here: 31.3 us
  blocking collectives  10 us (32%)
  starting transfers between devices  7.51 us (24%)
  waiting for transfers between devices  7.32 us (23%)
  Pallas kernels  5.84 us (18%)
  between operations  0.65 us (2%)
    all_to_all x1, blocking collectives, local(): returned = exchange(sending)  10 us
    all_to_all x1, starting transfers between devices, local(): near = exchange(outgoing)  7.29 us
    pallas_call x6, Pallas kernels, call(): pl.pallas_call(body, out_shape=tuple(outs), in_specs=[pl.BlockSpec(memory...  5.84 us
    all_to_all x1, waiting for transfers between devices, local(): near = exchange(outgoing)  5.47 us
    ppermute x1, waiting for transfers between devices, local(): came = lax.ppermute(leaving, 'expert', swap)  1.21 us
    ppermute x1, waiting for transfers between devices, local(): far = lax.ppermute(near, 'expert', swap)  0.64 us
  transfers between devices with their start and end apart: 3, of which 3 were waited for; matrix products, arithmetic and copies ran while one was open for 0% of the time, Pallas kernels for 8%

profile of v2, /device:TPU:0, one launch (start us, length us, event | category | flops | bytes accessed | tf_op | source)
XLA Modules:
  0.0 31.3 jit_solution(13029517324646272890)
XLA Ops:
  0.6 1.8 %shard_map.95 = bf16[8,2,4224]{2,1,0:T(2,128)(2,1)} custom-call(bf16[2,4096]{1,0:T(2,128)(2,1)} %tokens_ref.1, s32[2,2]{1,0:T(2,128)} %ids_ref.1, f32[2,2]{1,0:T(2,128)} %gates_ref.1, s32[2]{0:T(128)} %docs_ref.1), custom_call_target="tpu_custom_call" | custom-call | tf_op jit(solution)/shard_map/pallas_call | solution.py:26
  2.4 7.3 %all-to-all-start = ((bf16[8,2,4224]{2,1,0:T(2,128)(2,1)}), bf16[8,2,4224]{2,1,0:T(2,128)(2,1)S(1)}, u32[]{:S(2)}, u32[]{:S(2)}) async-start(bf16[8,2,4224]{2,1,0:T(2,128)(2,1)} %shard_map.95), calls=%async_computation | async-start | bytes 270336 | tf_op jit(solution)/shard_map/all_to_all | solution.py:206
  9.7 1.9 %shard_map.96 = (bf16[4096,128]{1,0:T(8,128)(2,1)S(1)}, bf16[4096,128]{1,0:T(8,128)(2,1)S(1)}, bf16[128,4096]{1,0:T(8,128)(2,1)S(1)}, f32[1,4096]{1,0:T(1,128)S(1)}) custom-call(bf16[4096,128]{1,0:T(8,128)(2,1)} %refs_0_.1, bf16[4096,128]{1,0:T(8,128)(2,1)} %refs_1_.1, bf16[128,4096]{1,0:T(8,128)(2,1)} %refs_2_.1, f32[1,4096]{1,0:T(1,128)} %bitcast.1), custom_call_target="tpu_custom_call" | custom-call | flops 10000000 | bytes 6324224 | tf_op jit(solution)/shard_map/pallas_call | solution.py:26
  11.6 5.5 %all-to-all-done.x_ref = bf16[8,2,4224]{2,1,0:T(2,128)(2,1)S(1)} async-done(((bf16[8,2,4224]{2,1,0:T(2,128)(2,1)}), bf16[8,2,4224]{2,1,0:T(2,128)(2,1)S(1)}, u32[]{:S(2)}, u32[]{:S(2)}) %all-to-all-start) | async-done | bytes 135200 | tf_op jit(solution)/shard_map/all_to_all | solution.py:206
  17.1 0.0 collective-permute-start
  17.1 0.7 %shard_map.97 = (f32[16,4096]{1,0:T(8,128)S(1)}, f32[2,128]{1,0:T(2,128)S(1)}) custom-call(bf16[8,2,4224]{2,1,0:T(2,128)(2,1)S(1)} %all-to-all-done.x_ref, bf16[4096,128]{1,0:T(8,128)(2,1)S(1)} %get-tuple-element.20.w_gate_ref, bf16[4096,128]{1,0:T(8,128)(2,1)S(1)} %get-tuple-element.21.w_up_ref, bf16[128,4096]{1,0:T(8,128)(2,1)S(1)} %get-tuple-element.22.w_down_ref, ...), custom_call_target="tpu_custom_call" | custom-call | tf_op jit(solution)/shard_map/pallas_call | solution.py:26
  17.8 0.6 %collective-permute-done.x_ref = bf16[8,2,4224]{2,1,0:T(2,128)(2,1)S(1)} collective-permute-done((bf16[8,2,4224]{2,1,0:T(2,128)(2,1)S(1)}, bf16[8,2,4224]{2,1,0:T(2,128)(2,1)S(1)}, u32[]{:S(2)}, u32[]{:S(2)}) %collective-permute-start) | collective-permute-done | bytes 135200 | tf_op jit(solution)/shard_map/ppermute | solution.py:217
  18.4 0.7 %shard_map.98 = (bf16[8,2,4224]{2,1,0:T(2,128)(2,1)S(1)}, f32[2,128]{1,0:T(2,128)S(1)}) custom-call(bf16[8,2,4224]{2,1,0:T(2,128)(2,1)S(1)} %collective-permute-done.x_ref, bf16[4096,128]{1,0:T(8,128)(2,1)S(1)} %get-tuple-element.20.w_gate_ref, bf16[4096,128]{1,0:T(8,128)(2,1)S(1)} %get-tuple-element.21.w_up_ref, ...), custom_call_target="tpu_custom_call" | custom-call | tf_op jit(solution)/shard_map/pallas_call | solution.py:26
  19.1 0.2 collective-permute-start.1
  19.3 1.2 %collective-permute-done.1.came_ref = bf16[8,2,4224]{2,1,0:T(2,128)(2,1)S(1)} collective-permute-done((bf16[8,2,4224]{2,1,0:T(2,128)(2,1)S(1)}, bf16[8,2,4224]{2,1,0:T(2,128)(2,1)S(1)}, u32[]{:S(2)}, u32[]{:S(2)}) %collective-permute-start.1) | collective-permute-done | bytes 135200 | tf_op jit(solution)/shard_map/ppermute | solution.py:226
  20.6 0.1 shard_map.99
  20.6 10.0 %all_to_all.10.came_ref = bf16[8,2,4224]{2,1,0:T(2,128)(2,1)S(1)} all-to-all(bf16[8,2,4224]{2,1,0:T(2,128)(2,1)S(1)} %shard_map.99), channel_id=1, replica_groups={{0,2,4,6,8,10,12,14},{1,3,5,7,9,11,13,15},{16,18,20,22,24,26,28,30},{17..., dimensions={0} | all-to-all | bytes 270336 | tf_op jit(solution)/shard_map/all_to_all | solution.py:228
  30.7 0.7 %shard_map.100 = (bf16[2,4096]{1,0:T(2,128)(2,1)}, f32[4]{0:T(128)}) custom-call(bf16[8,2,4224]{2,1,0:T(2,128)(2,1)S(1)} %all_to_all.10.came_ref, f32[2,128]{1,0:T(2,128)S(1)} %get-tuple-element.27.stat_ref), custom_call_target="tpu_custom_call" | custom-call | tf_op jit(solution)/shard_map/pallas_call | solution.py:26
Async XLA Ops:
  2.4 14.7 %all-to-all-start = ((bf16[8,2,4224]{2,1,0:T(2,128)(2,1)}), bf16[8,2,4224]{2,1,0:T(2,128)(2,1)S(1)}, u32[]{:S(2)}, u32[]{:S(2)}) async-start(bf16[8,2,4224]{2,1,0:T(2,128)(2,1)} %shard_map.95), calls=%async_computation | async-start | bytes 270336 | tf_op jit(solution)/shard_map/all_to_all | solution.py:206
  17.1 1.4 %collective-permute-start = (bf16[8,2,4224]{2,1,0:T(2,128)(2,1)S(1)}, bf16[8,2,4224]{2,1,0:T(2,128)(2,1)S(1)}, u32[]{:S(2)}, u32[]{:S(2)}) collective-permute-start(bf16[8,2,4224]{2,1,0:T(2,128)(2,1)S(1)} %all-to-all-done.x_ref), channel_id=1, source_target_pairs={{0,1},{1,0},{2,3},{3,2},{4,5},{5,4},{6,7},{7,6},{8,9},{9,8},{10,11... | collective-permute-start | bytes 405512 | tf_op jit(solution)/shard_map/ppermute | solution.py:217
  19.1 1.4 %collective-permute-start.1 = (bf16[8,2,4224]{2,1,0:T(2,128)(2,1)S(1)}, bf16[8,2,4224]{2,1,0:T(2,128)(2,1)S(1)}, u32[]{:S(2)}, u32[]{:S(2)}) collective-permute-start(bf16[8,2,4224]{2,1,0:T(2,128)(2,1)S(1)} %get-tuple-element.26), channel_id=1, source_target_pairs={{0,1},{1,0},{2,3},{3,2},{4,5},{5,4},{6,7},{7,6},{8,9},{9,8},{10,11... | collective-permute-start | bytes 405512 | tf_op jit(solution)/shard_map/ppermute | solution.py:226

commit v3 on v2

--- a/solution.py
+++ b/solution.py
@@ -10,7 +10,8 @@
 EXP_FLIGHT = 4
 LANES = 128
 VMEM_LIMIT = 24 * 1024 * 1024
-LOAD_FLOPS = 10_000_000
+PACK_FLOPS = 10**10
+PACK_BYTES = 3 * 10**7
 
 
 def split_pair(value):
@@ -73,18 +74,6 @@
         copy.wait()
 
 
-def load_body(*refs):
-    count = (len(refs) - 1) // 2
-    sems = refs[-1]
-    copies = [
-        pltpu.make_async_copy(refs[i], refs[count + i], sems.at[i]) for i in range(count)
-    ]
-    for copy in copies:
-        copy.start()
-    for copy in copies:
-        copy.wait()
-
-
 def expert_rows(spread, block, w_gate_ref, w_up_ref, w_down_ref, w_score_ref):
     blocks, each, total = block.shape
     rows = blocks * each
@@ -179,7 +168,12 @@
     half = members // 2
     total = width + LANES
     vmem, smem = pltpu.MemorySpace.VMEM, pltpu.MemorySpace.SMEM
-    alike = [list(range(side, members, 2)) for side in range(2)]
+    pairs = list(range(half))
+    alike = []
+    for side in range(2):
+        root = half // 2 + (1 - side) % half
+        order = [root] + [q for q in pairs if q != root]
+        alike.append([2 * q + (q + side) % 2 for q in order])
     swap = [(i, i ^ 1) for i in range(members)]
     exchange = functools.partial(
         lax.all_to_all, axis_name="expert", split_axis=0, concat_axis=0, axis_index_groups=alike, tiled=True
@@ -200,28 +194,23 @@
             pltpu.SMEM(doc_ids.shape, jnp.int32),
             pltpu.SemaphoreType.DMA((3 + half,)),
         ),
+        cost=pl.CostEstimate(flops=PACK_FLOPS, bytes_accessed=PACK_BYTES, transcendentals=0),
     )
     score_full = lax.all_gather(w_score, "tensor", axis=0, tiled=True) if parts > 1 else w_score
     weights = (w_gate, w_up, w_down, score_full.reshape(1, -1))
     near = exchange(outgoing)
+    flops = 3 * 2 * rows // 2 * width * w_gate.shape[1]
     size = sum(w.size * w.dtype.itemsize for w in weights)
-    weights = call(
-        load_body,
-        [jax.ShapeDtypeStruct(w.shape, w.dtype) for w in weights],
-        in_hbm(*weights),
-        [hbm] * len(weights),
-        cost=pl.CostEstimate(flops=LOAD_FLOPS, bytes_accessed=2 * size, transcendentals=0),
-        scratch=(pltpu.SemaphoreType.DMA((len(weights),)),),
-    )
-    near, *weights = lax.optimization_barrier((near, *weights))
+    cost = pl.CostEstimate(flops=flops, bytes_accessed=size + rows * width * 4, transcendentals=0)
     far = lax.ppermute(near, "expert", swap)
     kept, stat_near = call(
         functools.partial(first_body, spread),
         [jax.ShapeDtypeStruct((rows // 2, width), jnp.float32), stat],
         (near, *weights),
+        cost=cost,
     )
     leaving, stat_all = call(
-        functools.partial(second_body, spread), [packet, stat], (far, *weights, stat_near)
+        functools.partial(second_body, spread), [packet, stat], (far, *weights, stat_near), cost=cost
     )
     came = lax.ppermute(leaving, "expert", swap)
     (sending,) = call(add_body, [packet], (kept, came, stat_all))

time: 31.7 us -> 27.4 us (0.86)
  blocking collectives: 10 us -> 20.9 us
  starting transfers between devices: 7.51 us -> 1 us
  waiting for transfers between devices: 7.32 us -> 1.25 us
  Pallas kernels: 5.84 us -> 3.31 us
    all_to_all x0 -> x1, blocking collectives: none -> 11.3 us  [local(): near = exchange(outgoing)]
    all_to_all x1 -> x0, starting transfers between devices: 7.29 us -> none  [local(): near = exchange(outgoing)]
    all_to_all x1 -> x0, waiting for transfers between devices: 5.47 us -> none  [local(): near = exchange(outgoing)]
    pallas_call x6 -> x5, Pallas kernels: 5.84 us -> 3.31 us  [call(): pl.pallas_call(body, out_shape=tuple(outs), in_specs=[pl.BlockSpec(memory...]
    ppermute x1, starting transfers between devices: 0.01 us -> 0.57 us  [local(): far = lax.ppermute(near, 'expert', swap)]
    all_to_all x1, blocking collectives: 10 us -> 9.63 us  [local(): returned = exchange(sending)]
    ppermute x1, waiting for transfers between devices: 0.64 us -> 0.26 us  [local(): far = lax.ppermute(near, 'expert', swap)]
  transfers between devices with their start and end apart: 3 -> 2, of which waited for: 3 -> 2; matrix products, arithmetic and copies ran while one was open for 0% -> 0% of each run, Pallas kernels for 8% -> 3%
where the time goes in v3:
time: 27.4 us; the launch traced here: 27.2 us
  blocking collectives  20.9 us (76%)
  Pallas kernels  3.31 us (12%)
  waiting for transfers between devices  1.25 us (5%)
  starting transfers between devices  1 us (4%)
  between operations  0.68 us (2%)
    all_to_all x1, blocking collectives, local(): near = exchange(outgoing)  11.3 us
    all_to_all x1, blocking collectives, local(): returned = exchange(sending)  9.63 us
    pallas_call x5, Pallas kernels, call(): pl.pallas_call(body, out_shape=tuple(outs), in_specs=[pl.BlockSpec(memory...  3.31 us
    ppermute x1, waiting for transfers between devices, local(): came = lax.ppermute(leaving, 'expert', swap)  0.99 us
    ppermute x1, starting transfers between devices, local(): far = lax.ppermute(near, 'expert', swap)  0.57 us
  transfers between devices with their start and end apart: 2, of which 2 were waited for; matrix products, arithmetic and copies ran while one was open for 0% of the time, Pallas kernels for 3%

profile of v3, /device:TPU:0, one launch (start us, length us, event | category | flops | bytes accessed | tf_op | source)
XLA Modules:
  0.0 27.2 jit_solution(15466333967055980261)
XLA Ops:
  0.6 0.0 copy-start.2
  0.6 0.0 copy-start.1
  0.7 0.0 copy-start
  0.7 1.1 %shard_map.95 = bf16[8,2,4224]{2,1,0:T(2,128)(2,1)S(1)} custom-call(bf16[2,4096]{1,0:T(2,128)(2,1)} %tokens_ref.1, s32[2,2]{1,0:T(2,128)} %ids_ref.1, f32[2,2]{1,0:T(2,128)} %gates_ref.1, s32[2]{0:T(128)} %docs_ref.1), custom_call_target="tpu_custom_call" | custom-call | flops 10000000000 | bytes 30000000 | tf_op jit(solution)/shard_map/pallas_call | solution.py:27
  1.8 0.0 copy-start.3
  1.8 11.3 %all_to_all.10.x_ref = bf16[8,2,4224]{2,1,0:T(2,128)(2,1)S(1)} all-to-all(bf16[8,2,4224]{2,1,0:T(2,128)(2,1)S(1)} %shard_map.95), channel_id=1, replica_groups={{11,0,3,4,7,8,12,15},{9,1,2,5,6,10,13,14},{27,16,19,20,23,24,28,31},{25..., dimensions={0} | all-to-all | bytes 270336 | tf_op jit(solution)/shard_map/all_to_all | solution.py:201
  13.0 0.6 %collective-permute-start = (bf16[8,2,4224]{2,1,0:T(2,128)(2,1)S(1)}, bf16[8,2,4224]{2,1,0:T(2,128)(2,1)S(1)}, u32[]{:S(2)}, u32[]{:S(2)}) collective-permute-start(bf16[8,2,4224]{2,1,0:T(2,128)(2,1)S(1)} %all_to_all.10.x_ref), channel_id=1, source_target_pairs={{0,1},{1,0},{2,3},{3,2},{4,5},{5,4},{6,7},{7,6},{8,9},{9,8},{10,11... | collective-permute-start | bytes 405512 | tf_op jit(solution)/shard_map/ppermute | solution.py:205
  13.6 0.0 copy-done.2
  13.6 0.0 copy-done.1
  13.6 0.0 copy-done
  13.6 0.0 copy-done.3
  13.6 0.7 %shard_map.96 = (f32[16,4096]{1,0:T(8,128)S(1)}, f32[2,128]{1,0:T(2,128)S(1)}) custom-call(bf16[8,2,4224]{2,1,0:T(2,128)(2,1)S(1)} %all_to_all.10.x_ref, bf16[4096,128]{1,0:T(8,128)(2,1)S(1)} %copy-done, bf16[4096,128]{1,0:T(8,128)(2,1)S(1)} %copy-done.1, bf16[128,4096]{1,0:T(8,128)(2,1)S(1)} %copy-done.2, f32[1,4096]{1,0:T(1,128)S(1)} %bitcast.1), custom_call_target="tpu_custom_call" | custom-call | flops 50331648 | bytes 3686400 | tf_op jit(solution)/shard_map/pallas_call | solution.py:27
  14.3 0.3 collective-permute-done.x_ref
  14.6 0.7 %shard_map.97 = (bf16[8,2,4224]{2,1,0:T(2,128)(2,1)S(1)}, f32[2,128]{1,0:T(2,128)S(1)}) custom-call(bf16[8,2,4224]{2,1,0:T(2,128)(2,1)S(1)} %collective-permute-done.x_ref, bf16[4096,128]{1,0:T(8,128)(2,1)S(1)} %copy-done, bf16[4096,128]{1,0:T(8,128)(2,1)S(1)} %copy-done.1, bf16[128,4096]{1,0:T(8,128)(2,1)S(1)} %copy-done.2, f32[1,4096]{1,0:T(1,128)S(1)} %bitcast.2, ...), custom_call_target="tpu_custom_call" | custom-call | flops 50331648 | bytes 3686400 | tf_op jit(solution)/shard_map/pallas_call | solution.py:27
  15.3 0.4 %collective-permute-start.1 = (bf16[8,2,4224]{2,1,0:T(2,128)(2,1)S(1)}, bf16[8,2,4224]{2,1,0:T(2,128)(2,1)S(1)}, u32[]{:S(2)}, u32[]{:S(2)}) collective-permute-start(bf16[8,2,4224]{2,1,0:T(2,128)(2,1)S(1)} %get-tuple-element.8), channel_id=1, source_target_pairs={{0,1},{1,0},{2,3},{3,2},{4,5},{5,4},{6,7},{7,6},{8,9},{9,8},{10,11... | collective-permute-start | bytes 405512 | tf_op jit(solution)/shard_map/ppermute | solution.py:215
  15.8 1.0 %collective-permute-done.1.came_ref = bf16[8,2,4224]{2,1,0:T(2,128)(2,1)S(1)} collective-permute-done((bf16[8,2,4224]{2,1,0:T(2,128)(2,1)S(1)}, bf16[8,2,4224]{2,1,0:T(2,128)(2,1)S(1)}, u32[]{:S(2)}, u32[]{:S(2)}) %collective-permute-start.1) | collective-permute-done | bytes 135200 | tf_op jit(solution)/shard_map/ppermute | solution.py:215
  16.8 0.1 shard_map.98
  16.8 9.6 %all_to_all.11.came_ref = bf16[8,2,4224]{2,1,0:T(2,128)(2,1)S(1)} all-to-all(bf16[8,2,4224]{2,1,0:T(2,128)(2,1)S(1)} %shard_map.98), channel_id=1, replica_groups={{11,0,3,4,7,8,12,15},{9,1,2,5,6,10,13,14},{27,16,19,20,23,24,28,31},{25..., dimensions={0} | all-to-all | bytes 270336 | tf_op jit(solution)/shard_map/all_to_all | solution.py:217
  26.5 0.7 %shard_map.99 = (bf16[2,4096]{1,0:T(2,128)(2,1)}, f32[4]{0:T(128)}) custom-call(bf16[8,2,4224]{2,1,0:T(2,128)(2,1)S(1)} %all_to_all.11.came_ref, f32[2,128]{1,0:T(2,128)S(1)} %get-tuple-element.9.stat_ref), custom_call_target="tpu_custom_call" | custom-call | tf_op jit(solution)/shard_map/pallas_call | solution.py:27
Async XLA Ops:
  0.6 13.0 %copy-start.2 = (bf16[128,4096]{1,0:T(8,128)(2,1)S(1)}, bf16[128,4096]{1,0:T(8,128)(2,1)}, u32[]{:S(2)}) copy-start(bf16[128,4096]{1,0:T(8,128)(2,1)} %w_down_ref.3) | copy-start | bytes 3145732
  0.6 13.0 %copy-start.1 = (bf16[4096,128]{1,0:T(8,128)(2,1)S(1)}, bf16[4096,128]{1,0:T(8,128)(2,1)}, u32[]{:S(2)}) copy-start(bf16[4096,128]{1,0:T(8,128)(2,1)} %w_up_ref.3) | copy-start | bytes 3145732
  0.7 13.0 %copy-start = (bf16[4096,128]{1,0:T(8,128)(2,1)S(1)}, bf16[4096,128]{1,0:T(8,128)(2,1)}, u32[]{:S(2)}) copy-start(bf16[4096,128]{1,0:T(8,128)(2,1)} %w_gate_ref.3) | copy-start | bytes 3145732
  1.8 11.9 %copy-start.3 = (f32[4096]{0:T(1024)S(1)}, f32[4096]{0:T(1024)}, u32[]{:S(2)}) copy-start(f32[4096]{0:T(1024)} %param.15) | copy-start | bytes 49156
  13.0 1.6 %collective-permute-start = (bf16[8,2,4224]{2,1,0:T(2,128)(2,1)S(1)}, bf16[8,2,4224]{2,1,0:T(2,128)(2,1)S(1)}, u32[]{:S(2)}, u32[]{:S(2)}) collective-permute-start(bf16[8,2,4224]{2,1,0:T(2,128)(2,1)S(1)} %all_to_all.10.x_ref), channel_id=1, source_target_pairs={{0,1},{1,0},{2,3},{3,2},{4,5},{5,4},{6,7},{7,6},{8,9},{9,8},{10,11... | collective-permute-start | bytes 405512 | tf_op jit(solution)/shard_map/ppermute | solution.py:205
  15.3 1.4 %collective-permute-start.1 = (bf16[8,2,4224]{2,1,0:T(2,128)(2,1)S(1)}, bf16[8,2,4224]{2,1,0:T(2,128)(2,1)S(1)}, u32[]{:S(2)}, u32[]{:S(2)}) collective-permute-start(bf16[8,2,4224]{2,1,0:T(2,128)(2,1)S(1)} %get-tuple-element.8), channel_id=1, source_target_pairs={{0,1},{1,0},{2,3},{3,2},{4,5},{5,4},{6,7},{7,6},{8,9},{9,8},{10,11... | collective-permute-start | bytes 405512 | tf_op jit(solution)/shard_map/ppermute | solution.py:215

commit v4 on v3

--- a/solution.py
+++ b/solution.py
@@ -35,25 +35,34 @@
     )(*args)
 
 
+def exchange_groups(half):
+    middle = half // 2
+    exchanges = []
+    for roots in ((middle + 1, middle + 1), (middle + 1, middle)):
+        groups = []
+        for side, root in enumerate(roots):
+            order = [root] + [q for q in range(half) if q != root]
+            groups.append([2 * q + (int(q >= middle) ^ side) for q in order])
+        exchanges.append(groups)
+    return exchanges
+
+
 def in_hbm(*arrays):
     return tuple(pltpu.with_memory_space_constraint(a, pltpu.MemorySpace.HBM) for a in arrays)
 
 
-def pack_body(tokens_ref, ids_ref, gates_ref, docs_ref, out_ref, ids, gates, docs, sems):
+def pack_body(tokens_ref, ids_ref, gates_ref, docs_ref, out_ref, ids, gates, docs, held, sems):
     blocks, rows, _ = out_ref.shape
     width = tokens_ref.shape[1]
-    small = [
+    copies = [
         pltpu.make_async_copy(ids_ref, ids, sems.at[0]),
         pltpu.make_async_copy(gates_ref, gates, sems.at[1]),
         pltpu.make_async_copy(docs_ref, docs, sems.at[2]),
+        pltpu.make_async_copy(tokens_ref, held, sems.at[3]),
     ]
-    large = [
-        pltpu.make_async_copy(tokens_ref, out_ref.at[b, :, pl.ds(0, width)], sems.at[3 + b])
-        for b in range(blocks)
-    ]
-    for copy in small + large:
+    for copy in copies:
         copy.start()
-    for copy in small:
+    for copy in copies[:3]:
         copy.wait()
     lane = lax.broadcasted_iota(jnp.int32, (rows, LANES), 1)
     row = lax.broadcasted_iota(jnp.int32, (rows, LANES), 0)
@@ -70,8 +79,10 @@
     side = jnp.where(lane == 2 * EXP_FLIGHT, doc, side).astype(jnp.bfloat16)
     for b in range(blocks):
         out_ref[b, :, width:] = side
-    for copy in large:
-        copy.wait()
+    copies[3].wait()
+    block = held[...]
+    for b in range(blocks):
+        out_ref[b, :, :width] = block
 
 
 def expert_rows(spread, block, w_gate_ref, w_up_ref, w_down_ref, w_score_ref):
@@ -131,12 +142,17 @@
         out_ref[b, :, width:] = side
 
 
-def add_body(part_ref, came_ref, stat_ref, out_ref):
+def add_body(moves, part_ref, came_ref, stat_ref, out_ref):
     blocks, each, total = came_ref.shape
     width = total - LANES
     came = came_ref[...].reshape(blocks * each, total)
     added = part_ref[...] + came[:, :width].astype(jnp.float32)
-    out_ref[:, :, :width] = added.astype(jnp.bfloat16).reshape(blocks, each, width)
+    added = added.astype(jnp.bfloat16).reshape(blocks, each, width)
+    me = lax.axis_index("expert")
+    side = (me + me // blocks) % 2
+    for b in range(blocks):
+        to = moves[0][b] if moves[0][b] == moves[1][b] else jnp.where(side == 0, moves[0][b], moves[1][b])
+        out_ref[to, :, :width] = added[b]
     other = jnp.sum(came[:each, width:].astype(jnp.float32), axis=0, keepdims=True)
     side = side_rows(stat_ref[0:1] + other, each)
     for b in range(blocks):
@@ -168,15 +184,11 @@
     half = members // 2
     total = width + LANES
     vmem, smem = pltpu.MemorySpace.VMEM, pltpu.MemorySpace.SMEM
-    pairs = list(range(half))
-    alike = []
-    for side in range(2):
-        root = half // 2 + (1 - side) % half
-        order = [root] + [q for q in pairs if q != root]
-        alike.append([2 * q + (q + side) % 2 for q in order])
+    first_groups, second_groups = exchange_groups(half)
+    moves = [[b.index(m) for m in a] for a, b in zip(first_groups, second_groups)]
     swap = [(i, i ^ 1) for i in range(members)]
     exchange = functools.partial(
-        lax.all_to_all, axis_name="expert", split_axis=0, concat_axis=0, axis_index_groups=alike, tiled=True
+        lax.all_to_all, axis_name="expert", split_axis=0, concat_axis=0, tiled=True
     )
     packet = jax.ShapeDtypeStruct((half, tok_rows, total), jnp.bfloat16)
     stat = jax.ShapeDtypeStruct((2, LANES), jnp.float32)
@@ -192,13 +204,14 @@
             pltpu.SMEM(expert_ids.shape, jnp.int32),
             pltpu.SMEM(gate_weights.shape, jnp.float32),
             pltpu.SMEM(doc_ids.shape, jnp.int32),
-            pltpu.SemaphoreType.DMA((3 + half,)),
+            pltpu.VMEM(tokens.shape, tokens.dtype),
+            pltpu.SemaphoreType.DMA((4,)),
         ),
         cost=pl.CostEstimate(flops=PACK_FLOPS, bytes_accessed=PACK_BYTES, transcendentals=0),
     )
     score_full = lax.all_gather(w_score, "tensor", axis=0, tiled=True) if parts > 1 else w_score
     weights = (w_gate, w_up, w_down, score_full.reshape(1, -1))
-    near = exchange(outgoing)
+    near = exchange(outgoing, axis_index_groups=first_groups)
     flops = 3 * 2 * rows // 2 * width * w_gate.shape[1]
     size = sum(w.size * w.dtype.itemsize for w in weights)
     cost = pl.CostEstimate(flops=flops, bytes_accessed=size + rows * width * 4, transcendentals=0)
@@ -213,8 +226,8 @@
         functools.partial(second_body, spread), [packet, stat], (far, *weights, stat_near), cost=cost
     )
     came = lax.ppermute(leaving, "expert", swap)
-    (sending,) = call(add_body, [packet], (kept, came, stat_all))
-    returned = exchange(sending)
+    (sending,) = call(functools.partial(add_body, moves), [packet], (kept, came, stat_all))
+    returned = exchange(sending, axis_index_groups=second_groups)
     if parts == 1:
         return call(
             last_body,

time: 27.4 us -> 26.8 us (0.978)
  the two profiles are of different devices: /device:TPU:0 before, /device:TPU:1 now
where the time goes in v4:
time: 26.8 us; the launch traced here: 26.5 us
  blocking collectives  20.6 us (77%)
  Pallas kernels  3.12 us (12%)
  waiting for transfers between devices  1.81 us (7%)
  between operations  0.7 us (3%)
    all_to_all x1, blocking collectives, local(): near = exchange(outgoing, axis_index_groups=first_groups)  10.7 us
    all_to_all x1, blocking collectives, local(): returned = exchange(sending, axis_index_groups=second_groups)  9.89 us
    pallas_call x5, Pallas kernels, call(): pl.pallas_call(body, out_shape=tuple(outs), in_specs=[pl.BlockSpec(memory...  3.12 us
    ppermute x1, waiting for transfers between devices, local(): came = lax.ppermute(leaving, 'expert', swap)  1.21 us
    ppermute x1, waiting for transfers between devices, local(): far = lax.ppermute(near, 'expert', swap)  0.61 us
  transfers between devices with their start and end apart: 2, of which 2 were waited for; matrix products, arithmetic and copies ran while one was open for 0% of the time, Pallas kernels for 3%

profile of v4, /device:TPU:1, one launch (start us, length us, event | category | flops | bytes accessed | tf_op | source)
XLA Modules:
  0.0 26.5 jit_solution(6181819492522018829)
XLA Ops:
  0.6 0.0 copy-start.2
  0.6 0.0 copy-start.1
  0.7 0.0 copy-start
  0.7 0.9 %shard_map.95 = bf16[8,2,4224]{2,1,0:T(2,128)(2,1)S(1)} custom-call(bf16[2,4096]{1,0:T(2,128)(2,1)} %tokens_ref.1, s32[2,2]{1,0:T(2,128)} %ids_ref.1, f32[2,2]{1,0:T(2,128)} %gates_ref.1, s32[2]{0:T(128)} %docs_ref.1), custom_call_target="tpu_custom_call" | custom-call | flops 10000000000 | bytes 30000000 | tf_op jit(solution)/shard_map/pallas_call | solution.py:27
  1.6 0.0 copy-start.3
  1.6 10.7 %all_to_all.10.x_ref = bf16[8,2,4224]{2,1,0:T(2,128)(2,1)S(1)} all-to-all(bf16[8,2,4224]{2,1,0:T(2,128)(2,1)S(1)} %shard_map.95), channel_id=1, replica_groups={{11,0,2,4,6,9,13,15},{10,1,3,5,7,8,12,14},{27,16,18,20,22,25,29,31},{26..., dimensions={0} | all-to-all | bytes 270336 | tf_op jit(solution)/shard_map/all_to_all | solution.py:214
  12.3 0.0 collective-permute-start
  12.3 0.0 copy-done.2
  12.3 0.0 copy-done.1
  12.3 0.0 copy-done
  12.3 0.0 copy-done.3
  12.4 0.7 %shard_map.96 = (f32[16,4096]{1,0:T(8,128)S(1)}, f32[2,128]{1,0:T(2,128)S(1)}) custom-call(bf16[8,2,4224]{2,1,0:T(2,128)(2,1)S(1)} %all_to_all.10.x_ref, bf16[4096,128]{1,0:T(8,128)(2,1)S(1)} %copy-done, bf16[4096,128]{1,0:T(8,128)(2,1)S(1)} %copy-done.1, bf16[128,4096]{1,0:T(8,128)(2,1)S(1)} %copy-done.2, f32[1,4096]{1,0:T(1,128)S(1)} %bitcast.1), custom_call_target="tpu_custom_call" | custom-call | flops 50331648 | bytes 3686400 | tf_op jit(solution)/shard_map/pallas_call | solution.py:27
  13.1 0.6 %collective-permute-done.x_ref = bf16[8,2,4224]{2,1,0:T(2,128)(2,1)S(1)} collective-permute-done((bf16[8,2,4224]{2,1,0:T(2,128)(2,1)S(1)}, bf16[8,2,4224]{2,1,0:T(2,128)(2,1)S(1)}, u32[]{:S(2)}, u32[]{:S(2)}) %collective-permute-start) | collective-permute-done | bytes 135200 | tf_op jit(solution)/shard_map/ppermute | solution.py:218
  13.7 0.7 %shard_map.97 = (bf16[8,2,4224]{2,1,0:T(2,128)(2,1)S(1)}, f32[2,128]{1,0:T(2,128)S(1)}) custom-call(bf16[8,2,4224]{2,1,0:T(2,128)(2,1)S(1)} %collective-permute-done.x_ref, bf16[4096,128]{1,0:T(8,128)(2,1)S(1)} %copy-done, bf16[4096,128]{1,0:T(8,128)(2,1)S(1)} %copy-done.1, bf16[128,4096]{1,0:T(8,128)(2,1)S(1)} %copy-done.2, f32[1,4096]{1,0:T(1,128)S(1)} %bitcast.2, ...), custom_call_target="tpu_custom_call" | custom-call | flops 50331648 | bytes 3686400 | tf_op jit(solution)/shard_map/pallas_call | solution.py:27
  14.4 0.2 collective-permute-start.1
  14.6 1.2 %collective-permute-done.1.came_ref = bf16[8,2,4224]{2,1,0:T(2,128)(2,1)S(1)} collective-permute-done((bf16[8,2,4224]{2,1,0:T(2,128)(2,1)S(1)}, bf16[8,2,4224]{2,1,0:T(2,128)(2,1)S(1)}, u32[]{:S(2)}, u32[]{:S(2)}) %collective-permute-start.1) | collective-permute-done | bytes 135200 | tf_op jit(solution)/shard_map/ppermute | solution.py:228
  15.8 0.1 shard_map.98
  15.9 9.9 %all_to_all.11.came_ref = bf16[8,2,4224]{2,1,0:T(2,128)(2,1)S(1)} all-to-all(bf16[8,2,4224]{2,1,0:T(2,128)(2,1)S(1)} %shard_map.98), channel_id=1, replica_groups={{11,0,2,4,6,9,13,15},{8,1,3,5,7,10,12,14},{27,16,18,20,22,25,29,31},{24..., dimensions={0} | all-to-all | bytes 270336 | tf_op jit(solution)/shard_map/all_to_all | solution.py:230
  25.8 0.7 %shard_map.99 = (bf16[2,4096]{1,0:T(2,128)(2,1)}, f32[4]{0:T(128)}) custom-call(bf16[8,2,4224]{2,1,0:T(2,128)(2,1)S(1)} %all_to_all.11.came_ref, f32[2,128]{1,0:T(2,128)S(1)} %get-tuple-element.9.stat_ref), custom_call_target="tpu_custom_call" | custom-call | tf_op jit(solution)/shard_map/pallas_call | solution.py:27
Async XLA Ops:
  0.6 11.7 %copy-start.2 = (bf16[128,4096]{1,0:T(8,128)(2,1)S(1)}, bf16[128,4096]{1,0:T(8,128)(2,1)}, u32[]{:S(2)}) copy-start(bf16[128,4096]{1,0:T(8,128)(2,1)} %w_down_ref.3) | copy-start | bytes 3145732
  0.6 11.7 %copy-start.1 = (bf16[4096,128]{1,0:T(8,128)(2,1)S(1)}, bf16[4096,128]{1,0:T(8,128)(2,1)}, u32[]{:S(2)}) copy-start(bf16[4096,128]{1,0:T(8,128)(2,1)} %w_up_ref.3) | copy-start | bytes 3145732
  0.7 11.7 %copy-start = (bf16[4096,128]{1,0:T(8,128)(2,1)S(1)}, bf16[4096,128]{1,0:T(8,128)(2,1)}, u32[]{:S(2)}) copy-start(bf16[4096,128]{1,0:T(8,128)(2,1)} %w_gate_ref.3) | copy-start | bytes 3145732
  1.6 10.8 %copy-start.3 = (f32[4096]{0:T(1024)S(1)}, f32[4096]{0:T(1024)}, u32[]{:S(2)}) copy-start(f32[4096]{0:T(1024)} %param.15) | copy-start | bytes 49156
  12.3 1.4 %collective-permute-start = (bf16[8,2,4224]{2,1,0:T(2,128)(2,1)S(1)}, bf16[8,2,4224]{2,1,0:T(2,128)(2,1)S(1)}, u32[]{:S(2)}, u32[]{:S(2)}) collective-permute-start(bf16[8,2,4224]{2,1,0:T(2,128)(2,1)S(1)} %all_to_all.10.x_ref), channel_id=1, source_target_pairs={{0,1},{1,0},{2,3},{3,2},{4,5},{5,4},{6,7},{7,6},{8,9},{9,8},{10,11... | collective-permute-start | bytes 405512 | tf_op jit(solution)/shard_map/ppermute | solution.py:218
  14.4 1.4 %collective-permute-start.1 = (bf16[8,2,4224]{2,1,0:T(2,128)(2,1)S(1)}, bf16[8,2,4224]{2,1,0:T(2,128)(2,1)S(1)}, u32[]{:S(2)}, u32[]{:S(2)}) collective-permute-start(bf16[8,2,4224]{2,1,0:T(2,128)(2,1)S(1)} %get-tuple-element.8), channel_id=1, source_target_pairs={{0,1},{1,0},{2,3},{3,2},{4,5},{5,4},{6,7},{7,6},{8,9},{9,8},{10,11... | collective-permute-start | bytes 405512 | tf_op jit(solution)/shard_map/ppermute | solution.py:228

commit v5 on v4

--- a/solution.py
+++ b/solution.py
@@ -62,6 +62,10 @@
     ]
     for copy in copies:
         copy.start()
+    copies[3].wait()
+    block = held[...]
+    for b in range(blocks):
+        out_ref[b, :, :width] = block
     for copy in copies[:3]:
         copy.wait()
     lane = lax.broadcasted_iota(jnp.int32, (rows, LANES), 1)
@@ -79,34 +83,64 @@
     side = jnp.where(lane == 2 * EXP_FLIGHT, doc, side).astype(jnp.bfloat16)
     for b in range(blocks):
         out_ref[b, :, width:] = side
-    copies[3].wait()
-    block = held[...]
-    for b in range(blocks):
-        out_ref[b, :, :width] = block
-
-
-def expert_rows(spread, block, w_gate_ref, w_up_ref, w_down_ref, w_score_ref):
-    blocks, each, total = block.shape
+
+
+def hidden_rows(held, w_gate, w_up):
+    gate = jnp.dot(held, w_gate, preferred_element_type=jnp.float32)
+    up = jnp.dot(held, w_up, preferred_element_type=jnp.float32)
+    return (gate / (1.0 + jnp.exp(-gate)) * up).astype(jnp.bfloat16)
+
+
+def score_rows(w_down, score):
+    row = lax.broadcasted_iota(jnp.int32, (8, score.shape[1]), 0)
+    pieces = jnp.zeros((8, score.shape[1]), jnp.float32)
+    rest = score
+    for i in range(3):
+        piece = rest.astype(jnp.bfloat16).astype(jnp.float32)
+        pieces = jnp.where(row == i, piece, pieces)
+        rest = rest - piece
+    added = lax.dot_general(
+        pieces.astype(jnp.bfloat16), w_down, (((1,), (1,)), ((), ())), preferred_element_type=jnp.float32
+    )
+    return jnp.sum(added, axis=0, keepdims=True)
+
+
+def hidden_body(spread, doc_total, x_ref, *refs):
+    gates, ups = refs[0:2], refs[2:4]
+    hidden_ref, weight_ref, stat_ref = refs[4:]
+    blocks, each, total = x_ref.shape
     rows = blocks * each
     width = total - LANES
-    flat = block.reshape(rows, total)
+    flat = x_ref[...].reshape(rows, total)
     held = flat[:, :width]
     side = flat[:, width:].astype(jnp.float32)
-    gate = jnp.dot(held, w_gate_ref[...], preferred_element_type=jnp.float32)
-    up = jnp.dot(held, w_up_ref[...], preferred_element_type=jnp.float32)
-    hidden = (gate / (1.0 + jnp.exp(-gate)) * up).astype(jnp.bfloat16)
-    part = jnp.dot(hidden, w_down_ref[...], preferred_element_type=jnp.float32)
     own = lax.axis_index("expert") // spread
     lane = lax.broadcasted_iota(jnp.int32, (rows, LANES), 1)
     mine = (lane == own) | (lane == own + EXP_FLIGHT)
     weight = jnp.sum(jnp.where(mine, side, 0.0), axis=1, keepdims=True)
     doc = jnp.sum(jnp.where(lane == 2 * EXP_FLIGHT, side, 0.0), axis=1, keepdims=True)
-    part = part * weight
-    projected = jnp.sum(part * w_score_ref[...], axis=1, keepdims=True)
-    hits = doc == lane.astype(jnp.float32)
-    sums = jnp.sum(jnp.where(hits, projected, 0.0), axis=0, keepdims=True)
-    counts = jnp.sum(jnp.where(hits, 1.0, 0.0), axis=0, keepdims=True)
-    return part, sums, counts
+    weight_ref[...] = jnp.broadcast_to(weight, (rows, LANES))
+    stat_ref[...] = jnp.zeros(stat_ref.shape, jnp.float32)
+    hits = jnp.where(doc == lane.astype(jnp.float32), 1.0, 0.0)
+    stat_ref[doc_total : doc_total + 1, :LANES] = jnp.sum(hits, axis=0, keepdims=True)
+    units = gates[0].shape[1]
+    for i in range(2):
+        hidden = hidden_rows(held, gates[i][...], ups[i][...])
+        hidden_ref[:, i * units : (i + 1) * units] = hidden
+        hidden = hidden.astype(jnp.float32) * weight
+        for d in range(doc_total):
+            chosen = jnp.where(doc == float(d), hidden, 0.0)
+            stat_ref[d : d + 1, i * units : (i + 1) * units] = jnp.sum(chosen, axis=0, keepdims=True)
+
+
+def down_body(hidden_ref, weight_ref, own_ref, other_ref, score_ref, out_ref, reach_ref):
+    units = own_ref.shape[0]
+    part = jnp.dot(hidden_ref[:, :units], own_ref[...], preferred_element_type=jnp.float32)
+    part += jnp.dot(hidden_ref[:, units:], other_ref[...], preferred_element_type=jnp.float32)
+    out_ref[...] = (part * weight_ref[:, 0:1]).astype(jnp.bfloat16)
+    score = score_ref[...]
+    reach_ref[:, :units] = score_rows(own_ref[...], score)
+    reach_ref[:, units:] = score_rows(other_ref[...], score)
 
 
 def side_rows(sums, rows):
@@ -116,45 +150,28 @@
     return side.astype(jnp.bfloat16)
 
 
-def first_body(spread, x_ref, w_gate_ref, w_up_ref, w_down_ref, w_score_ref, part_ref, stat_ref):
-    part, sums, counts = expert_rows(
-        spread, x_ref[...], w_gate_ref, w_up_ref, w_down_ref, w_score_ref
-    )
-    part_ref[...] = part
-    stat_ref[0:1] = sums
-    stat_ref[1:2] = counts
-
-
-def second_body(
-    spread, x_ref, w_gate_ref, w_up_ref, w_down_ref, w_score_ref, before_ref, out_ref, stat_ref
-):
-    blocks, each, total = x_ref.shape
+def join_body(moves, doc_total, part_ref, reach_ref, stat_ref, came_ref, out_ref, total_ref):
+    blocks, each, total = out_ref.shape
     width = total - LANES
-    part, sums, counts = expert_rows(
-        spread, x_ref[...], w_gate_ref, w_up_ref, w_down_ref, w_score_ref
-    )
-    sums = sums + before_ref[0:1]
-    stat_ref[0:1] = sums
-    stat_ref[1:2] = counts + before_ref[1:2]
-    out_ref[:, :, :width] = part.astype(jnp.bfloat16).reshape(blocks, each, width)
+    part = part_ref[...].reshape(blocks, each, width)
+    me = lax.axis_index("expert")
+    group = (me + me // blocks) % 2
+    for b in range(blocks):
+        to = moves[0][b]
+        if moves[1][b] != to:
+            to = jnp.where(group == 0, to, moves[1][b])
+        out_ref[to, :, :width] = part[b]
+    units = reach_ref.shape[1] // 2
+    came = came_ref[...]
+    docs = stat_ref[...] + jnp.concatenate([came[:, units:], came[:, :units]], axis=1)
+    column = jnp.sum(docs * reach_ref[...], axis=1, keepdims=True)
+    row = lax.broadcasted_iota(jnp.int32, (docs.shape[0], LANES), 0)
+    lane = lax.broadcasted_iota(jnp.int32, (docs.shape[0], LANES), 1)
+    sums = jnp.sum(jnp.where((row == lane) & (row < doc_total), column, 0.0), axis=0, keepdims=True)
+    total_ref[0:1] = sums
+    counts = slice(doc_total, doc_total + 1)
+    total_ref[1:2] = stat_ref[counts, :LANES] + came_ref[counts, :LANES]
     side = side_rows(sums, each)
-    for b in range(blocks):
-        out_ref[b, :, width:] = side
-
-
-def add_body(moves, part_ref, came_ref, stat_ref, out_ref):
-    blocks, each, total = came_ref.shape
-    width = total - LANES
-    came = came_ref[...].reshape(blocks * each, total)
-    added = part_ref[...] + came[:, :width].astype(jnp.float32)
-    added = added.astype(jnp.bfloat16).reshape(blocks, each, width)
-    me = lax.axis_index("expert")
-    side = (me + me // blocks) % 2
-    for b in range(blocks):
-        to = moves[0][b] if moves[0][b] == moves[1][b] else jnp.where(side == 0, moves[0][b], moves[1][b])
-        out_ref[to, :, :width] = added[b]
-    other = jnp.sum(came[:each, width:].astype(jnp.float32), axis=0, keepdims=True)
-    side = side_rows(stat_ref[0:1] + other, each)
     for b in range(blocks):
         out_ref[b, :, width:] = side
 
@@ -169,9 +186,7 @@
     totals = jnp.sum(summed[:, width:], axis=0, keepdims=True)
     ratio = totals / stat_ref[1:2]
     scores = 1.0 / (1.0 + jnp.exp(-ratio))
-    lane = lax.broadcasted_iota(jnp.int32, (1, LANES), 1)
-    for d in range(scores_ref.shape[0]):
-        scores_ref[d] = jnp.sum(jnp.where(lane == d, scores, 0.0))
+    scores_ref[...] = scores[0, : scores_ref.shape[0]]
 
 
 def local(tokens, expert_ids, gate_weights, doc_ids, w_gate, w_up, w_down, w_score):
@@ -210,23 +225,39 @@
         cost=pl.CostEstimate(flops=PACK_FLOPS, bytes_accessed=PACK_BYTES, transcendentals=0),
     )
     score_full = lax.all_gather(w_score, "tensor", axis=0, tiled=True) if parts > 1 else w_score
-    weights = (w_gate, w_up, w_down, score_full.reshape(1, -1))
+    units = w_gate.shape[1]
+    other = [lax.ppermute(w, "expert", swap) for w in (w_gate, w_up, w_down)]
     near = exchange(outgoing, axis_index_groups=first_groups)
-    flops = 3 * 2 * rows // 2 * width * w_gate.shape[1]
-    size = sum(w.size * w.dtype.itemsize for w in weights)
-    cost = pl.CostEstimate(flops=flops, bytes_accessed=size + rows * width * 4, transcendentals=0)
-    far = lax.ppermute(near, "expert", swap)
-    kept, stat_near = call(
-        functools.partial(first_body, spread),
-        [jax.ShapeDtypeStruct((rows // 2, width), jnp.float32), stat],
-        (near, *weights),
+    cost = pl.CostEstimate(
+        flops=2 * rows * width * units, bytes_accessed=12 * width * units, transcendentals=0
+    )
+    sums = jax.ShapeDtypeStruct((-(-(doc_total + 1) // 8) * 8, 2 * units), jnp.float32)
+    score_full = score_full.reshape(1, -1)
+    hidden, weight, sums_near = call(
+        functools.partial(hidden_body, spread, doc_total),
+        [
+            jax.ShapeDtypeStruct((rows // 2, 2 * units), jnp.bfloat16),
+            jax.ShapeDtypeStruct((rows // 2, LANES), jnp.float32),
+            sums,
+        ],
+        (near, w_gate, other[0], w_up, other[1]),
         cost=cost,
     )
-    leaving, stat_all = call(
-        functools.partial(second_body, spread), [packet, stat], (far, *weights, stat_near), cost=cost
-    )
-    came = lax.ppermute(leaving, "expert", swap)
-    (sending,) = call(functools.partial(add_body, moves), [packet], (kept, came, stat_all))
+    sums_far = lax.ppermute(sums_near, "expert", swap)
+    part, reach = call(
+        down_body,
+        [
+            jax.ShapeDtypeStruct((rows // 2, width), jnp.bfloat16),
+            jax.ShapeDtypeStruct((1, 2 * units), jnp.float32),
+        ],
+        (hidden, weight, w_down, other[2], score_full),
+        cost=cost,
+    )
+    sending, stat_all = call(
+        functools.partial(join_body, moves, doc_total),
+        [packet, stat],
+        (part, reach, sums_near, sums_far),
+    )
     returned = exchange(sending, axis_index_groups=second_groups)
     if parts == 1:
         return call(
@@ -237,7 +268,7 @@
             ],
             (returned, stat_all),
             None,
-            [vmem, smem],
+            [vmem, vmem],
         )
     summed = jnp.sum(returned.astype(jnp.float32), axis=0)
     mixed = lax.psum_scatter(summed[:, :width], "tensor", scatter_dimension=1, tiled=True)

time: 26.8 us -> 25.9 us (0.966)
  waiting for transfers between devices: 1.81 us -> 0.01 us
  starting transfers between devices: 0.22 us -> 0.72 us
  local copies, waits for them, and re-layouts: 0.02 us -> 0.42 us
    ppermute x2 -> x4, waiting for transfers between devices: 1.81 us -> 0.01 us  [the longest x3 0.01 us: local(): other = [lax.ppermute(w, 'expert', swap) for w in (w_gate, w_up, w_down)]]
    ppermute x2 -> x4, starting transfers between devices: 0.22 us -> 0.72 us  [the longest x3 0.65 us: local(): other = [lax.ppermute(w, 'expert', swap) for w in (w_gate, w_up, w_down)]]
    all_to_all x1, blocking collectives: 9.89 us -> 9.43 us  [local(): returned = exchange(sending, axis_index_groups=second_groups)]
    unnamed x8, local copies, waits for them, and re-layouts: 0.02 us -> 0.42 us
    all_to_all x1, blocking collectives: 10.7 us -> 11.1 us  [local(): near = exchange(outgoing, axis_index_groups=first_groups)]
  transfers between devices with their start and end apart: 2 -> 4, of which waited for: 2 -> 0; matrix products, arithmetic and copies ran while one was open for 0% -> 0% of each run, Pallas kernels for 3% -> 9%
where the time goes in v5:
time: 25.9 us; the launch traced here: 25.6 us
  blocking collectives  20.5 us (79%)
  Pallas kernels  3.18 us (12%)
  starting transfers between devices  0.72 us (3%)
  between operations  0.71 us (3%)
  local copies, waits for them, and re-layouts  0.42 us (2%)
    all_to_all x1, blocking collectives, local(): near = exchange(outgoing, axis_index_groups=first_groups)  11.1 us
    all_to_all x1, blocking collectives, local(): returned = exchange(sending, axis_index_groups=second_groups)  9.43 us
    pallas_call x5, Pallas kernels, call(): pl.pallas_call(body, out_shape=tuple(outs), in_specs=[pl.BlockSpec(memory...  3.18 us
    ppermute x3, starting transfers between devices, local(): other = [lax.ppermute(w, 'expert', swap) for w in (w_gate, w_up, w_down)]  0.65 us
  transfers between devices with their start and end apart: 4, of which 0 were waited for; matrix products, arithmetic and copies ran while one was open for 0% of the time, Pallas kernels for 9%

profile of v5, /device:TPU:1, one launch (start us, length us, event | category | flops | bytes accessed | tf_op | source)
XLA Modules:
  0.0 25.6 jit_solution(1283410364784263446)
XLA Ops:
  0.6 0.0 copy-start
  0.6 0.0 copy-start.1
  0.7 0.1 collective-permute-start
  0.7 0.5 %collective-permute-start.1 = (bf16[4096,128]{1,0:T(8,128)(2,1)}, bf16[4096,128]{1,0:T(8,128)(2,1)S(1)}, u32[]{:S(2)}, u32[]{:S(2)}) collective-permute-start(bf16[4096,128]{1,0:T(8,128)(2,1)} %refs_2_.1), channel_id=1, source_target_pairs={{0,1},{1,0},{2,3},{3,2},{4,5},{5,4},{6,7},{7,6},{8,9},{9,8},{10,11... | collective-permute-start | bytes 3145736 | tf_op jit(solution)/shard_map/ppermute | solution.py:229
  1.2 0.1 collective-permute-start.2
  1.3 0.8 %shard_map.95 = bf16[8,2,4224]{2,1,0:T(2,128)(2,1)S(1)} custom-call(bf16[2,4096]{1,0:T(2,128)(2,1)} %tokens_ref.1, s32[2,2]{1,0:T(2,128)} %ids_ref.1, f32[2,2]{1,0:T(2,128)} %gates_ref.1, s32[2]{0:T(128)} %docs_ref.1), custom_call_target="tpu_custom_call" | custom-call | flops 10000000000 | bytes 30000000 | tf_op jit(solution)/shard_map/pallas_call | solution.py:27
  2.1 11.1 %all_to_all.10.x_ref = bf16[8,2,4224]{2,1,0:T(2,128)(2,1)S(1)} all-to-all(bf16[8,2,4224]{2,1,0:T(2,128)(2,1)S(1)} %shard_map.95), channel_id=1, replica_groups={{11,0,2,4,6,9,13,15},{10,1,3,5,7,8,12,14},{27,16,18,20,22,25,29,31},{26..., dimensions={0} | all-to-all | bytes 270336 | tf_op jit(solution)/shard_map/all_to_all | solution.py:230
  13.2 0.0 copy-start.2
  13.2 0.0 collective-permute-done.refs_1_
  13.2 0.0 collective-permute-done.1.refs_3_
  13.2 0.0 copy-done
  13.2 0.0 copy-done.1
  13.2 0.0 copy-start.3
  13.3 0.7 %shard_map.96 = (bf16[16,256]{1,0:T(8,128)(2,1)S(1)}, f32[16,128]{1,0:T(8,128)S(1)}, f32[8,256]{1,0:T(8,128)S(1)}) custom-call(bf16[8,2,4224]{2,1,0:T(2,128)(2,1)S(1)} %all_to_all.10.x_ref, bf16[4096,128]{1,0:T(8,128)(2,1)S(1)} %copy-done, bf16[4096,128]{1,0:T(8,128)(2,1)S(1)} %collective-permute-done.refs_1_, bf16[4096,128]{1,0:T(8,128)(2,1)S(1)} %copy-done.1, ...), custom_call_target="tpu_custom_call" | custom-call | flops 33554432 | bytes 6291456 | tf_op jit(solution)/shard_map/pallas_call | solution.py:27
  13.9 0.1 collective-permute-start.3
  14.0 0.0 collective-permute-done.2.other_ref
  14.0 0.4 %copy-done.2 = bf16[128,4096]{1,0:T(8,128)(2,1)S(1)} copy-done((bf16[128,4096]{1,0:T(8,128)(2,1)S(1)}, bf16[128,4096]{1,0:T(8,128)(2,1)}, u32[]{:S(2)}) %copy-start.2) | copy-done | bytes 1048600
  14.4 0.0 copy-done.3
  14.4 0.9 %shard_map.97 = (bf16[16,4096]{1,0:T(8,128)(2,1)S(1)}, f32[1,256]{1,0:T(1,128)S(1)}) custom-call(bf16[16,256]{1,0:T(8,128)(2,1)S(1)} %get-tuple-element.9.hidden_ref, f32[16,128]{1,0:T(8,128)S(1)} %get-tuple-element.10.weight_ref, bf16[128,4096]{1,0:T(8,128)(2,1)S(1)} %copy-done.2, bf16[128,4096]{1,0:T(8,128)(2,1)S(1)} %collective-permute-done.2.other_ref, ...), custom_call_target="tpu_custom_call" | custom-call | flops 33554432 | bytes 6291456 | tf_op jit(solution)/shard_map/pallas_call | solution.py:27
  15.3 0.0 collective-permute-done.3.came_ref
  15.4 0.1 shard_map.98
  15.5 9.4 %all_to_all.11.came_ref = bf16[8,2,4224]{2,1,0:T(2,128)(2,1)S(1)} all-to-all(bf16[8,2,4224]{2,1,0:T(2,128)(2,1)S(1)} %get-tuple-element.14), channel_id=1, replica_groups={{11,0,2,4,6,9,13,15},{8,1,3,5,7,10,12,14},{27,16,18,20,22,25,29,31},{24..., dimensions={0} | all-to-all | bytes 270336 | tf_op jit(solution)/shard_map/all_to_all | solution.py:261
  24.9 0.6 %shard_map.99 = (bf16[2,4096]{1,0:T(2,128)(2,1)}, f32[4]{0:T(128)}) custom-call(bf16[8,2,4224]{2,1,0:T(2,128)(2,1)S(1)} %all_to_all.11.came_ref, f32[2,128]{1,0:T(2,128)S(1)} %get-tuple-element.15.stat_ref), custom_call_target="tpu_custom_call" | custom-call | tf_op jit(solution)/shard_map/pallas_call | solution.py:27
Async XLA Ops:
  0.6 12.6 %copy-start = (bf16[4096,128]{1,0:T(8,128)(2,1)S(1)}, bf16[4096,128]{1,0:T(8,128)(2,1)}, u32[]{:S(2)}) copy-start(bf16[4096,128]{1,0:T(8,128)(2,1)} %refs_0_.1) | copy-start | bytes 3145732
  0.6 12.6 %copy-start.1 = (bf16[4096,128]{1,0:T(8,128)(2,1)S(1)}, bf16[4096,128]{1,0:T(8,128)(2,1)}, u32[]{:S(2)}) copy-start(bf16[4096,128]{1,0:T(8,128)(2,1)} %refs_2_.1) | copy-start | bytes 3145732
  0.7 12.6 %collective-permute-start = (bf16[4096,128]{1,0:T(8,128)(2,1)}, bf16[4096,128]{1,0:T(8,128)(2,1)S(1)}, u32[]{:S(2)}, u32[]{:S(2)}) collective-permute-start(bf16[4096,128]{1,0:T(8,128)(2,1)} %refs_0_.1), channel_id=1, source_target_pairs={{0,1},{1,0},{2,3},{3,2},{4,5},{5,4},{6,7},{7,6},{8,9},{9,8},{10,11... | collective-permute-start | bytes 3145736 | tf_op jit(solution)/shard_map/ppermute | solution.py:229
  0.7 12.5 %collective-permute-start.1 = (bf16[4096,128]{1,0:T(8,128)(2,1)}, bf16[4096,128]{1,0:T(8,128)(2,1)S(1)}, u32[]{:S(2)}, u32[]{:S(2)}) collective-permute-start(bf16[4096,128]{1,0:T(8,128)(2,1)} %refs_2_.1), channel_id=1, source_target_pairs={{0,1},{1,0},{2,3},{3,2},{4,5},{5,4},{6,7},{7,6},{8,9},{9,8},{10,11... | collective-permute-start | bytes 3145736 | tf_op jit(solution)/shard_map/ppermute | solution.py:229
  1.2 12.8 %collective-permute-start.2 = (bf16[128,4096]{1,0:T(8,128)(2,1)}, bf16[128,4096]{1,0:T(8,128)(2,1)S(1)}, u32[]{:S(2)}, u32[]{:S(2)}) collective-permute-start(bf16[128,4096]{1,0:T(8,128)(2,1)} %own_ref.1), channel_id=1, source_target_pairs={{0,1},{1,0},{2,3},{3,2},{4,5},{5,4},{6,7},{7,6},{8,9},{9,8},{10,11... | collective-permute-start | bytes 3145736 | tf_op jit(solution)/shard_map/ppermute | solution.py:229
  13.2 1.2 %copy-start.2 = (bf16[128,4096]{1,0:T(8,128)(2,1)S(1)}, bf16[128,4096]{1,0:T(8,128)(2,1)}, u32[]{:S(2)}) copy-start(bf16[128,4096]{1,0:T(8,128)(2,1)} %own_ref.1) | copy-start | bytes 3145732
  13.2 1.2 %copy-start.3 = (f32[4096]{0:T(1024)S(1)}, f32[4096]{0:T(1024)}, u32[]{:S(2)}) copy-start(f32[4096]{0:T(1024)} %param.15) | copy-start | bytes 49156
  13.9 1.4 %collective-permute-start.3 = (f32[8,256]{1,0:T(8,128)S(1)}, f32[8,256]{1,0:T(8,128)S(1)}, u32[]{:S(2)}, u32[]{:S(2)}) collective-permute-start(f32[8,256]{1,0:T(8,128)S(1)} %get-tuple-element.13.stat_ref), channel_id=1, source_target_pairs={{0,1},{1,0},{2,3},{3,2},{4,5},{5,4},{6,7},{7,6},{8,9},{9,8},{10,11... | collective-permute-start | bytes 24584 | tf_op jit(solution)/shard_map/ppermute | solution.py:246

commit v6 on v5

--- a/solution.py
+++ b/solution.py
@@ -10,8 +10,8 @@
 EXP_FLIGHT = 4
 LANES = 128
 VMEM_LIMIT = 24 * 1024 * 1024
-PACK_FLOPS = 10**10
-PACK_BYTES = 3 * 10**7
+OPEN_FLOPS = 10**10
+OPEN_BYTES = 3 * 10**7
 
 
 def split_pair(value):
@@ -51,37 +51,29 @@
     return tuple(pltpu.with_memory_space_constraint(a, pltpu.MemorySpace.HBM) for a in arrays)
 
 
-def pack_body(tokens_ref, ids_ref, gates_ref, docs_ref, out_ref, ids, gates, docs, held, sems):
+def open_body(out_ref):
+    out_ref[...] = jnp.zeros(out_ref.shape, out_ref.dtype)
+
+
+def pack_body(opened_ref, tokens_ref, ids_ref, gates_ref, docs_ref, out_ref):
     blocks, rows, _ = out_ref.shape
     width = tokens_ref.shape[1]
-    copies = [
-        pltpu.make_async_copy(ids_ref, ids, sems.at[0]),
-        pltpu.make_async_copy(gates_ref, gates, sems.at[1]),
-        pltpu.make_async_copy(docs_ref, docs, sems.at[2]),
-        pltpu.make_async_copy(tokens_ref, held, sems.at[3]),
-    ]
-    for copy in copies:
-        copy.start()
-    copies[3].wait()
-    block = held[...]
+    lane = lax.broadcasted_iota(jnp.int32, (rows, LANES), 1)
+    weight = jnp.zeros((rows, LANES), jnp.float32)
+    for k in range(ids_ref.shape[1]):
+        named = ids_ref[:, k : k + 1]
+        hit = (lane == named) | (lane == named + EXP_FLIGHT)
+        weight = jnp.where(hit, gates_ref[:, k : k + 1], weight)
+    high, low = split_pair(weight)
+    side = jnp.where(lane < EXP_FLIGHT, high, low)
+    row = lax.broadcasted_iota(jnp.int32, (rows, rows), 0)
+    column = lax.broadcasted_iota(jnp.int32, (rows, rows), 1)
+    docs = docs_ref[...].astype(jnp.float32).reshape(1, rows)
+    doc = jnp.sum(jnp.where(row == column, docs, 0.0), axis=1, keepdims=True)
+    side = jnp.where(lane == 2 * EXP_FLIGHT, doc, side).astype(jnp.bfloat16)
+    block = tokens_ref[...]
     for b in range(blocks):
         out_ref[b, :, :width] = block
-    for copy in copies[:3]:
-        copy.wait()
-    lane = lax.broadcasted_iota(jnp.int32, (rows, LANES), 1)
-    row = lax.broadcasted_iota(jnp.int32, (rows, LANES), 0)
-    weight = jnp.zeros((rows, LANES), jnp.float32)
-    doc = jnp.zeros((rows, LANES), jnp.float32)
-    for r in range(rows):
-        for k in range(ids.shape[1]):
-            named = ids[r, k]
-            hit = (row == r) & ((lane == named) | (lane == named + EXP_FLIGHT))
-            weight = jnp.where(hit, gates[r, k], weight)
-        doc = jnp.where(row == r, docs[r].astype(jnp.float32), doc)
-    high, low = split_pair(weight)
-    side = jnp.where(lane < EXP_FLIGHT, high, low)
-    side = jnp.where(lane == 2 * EXP_FLIGHT, doc, side).astype(jnp.bfloat16)
-    for b in range(blocks):
         out_ref[b, :, width:] = side
 
 
@@ -210,19 +202,17 @@
 
     hbm = pltpu.MemorySpace.HBM
 
+    (opened,) = call(
+        open_body,
+        [jax.ShapeDtypeStruct((8, LANES), jnp.float32)],
+        (),
+        cost=pl.CostEstimate(flops=OPEN_FLOPS, bytes_accessed=OPEN_BYTES, transcendentals=0),
+    )
     (outgoing,) = call(
         pack_body,
         [packet],
-        in_hbm(tokens, expert_ids, gate_weights, doc_ids),
-        [hbm] * 4,
-        scratch=(
-            pltpu.SMEM(expert_ids.shape, jnp.int32),
-            pltpu.SMEM(gate_weights.shape, jnp.float32),
-            pltpu.SMEM(doc_ids.shape, jnp.int32),
-            pltpu.VMEM(tokens.shape, tokens.dtype),
-            pltpu.SemaphoreType.DMA((4,)),
-        ),
-        cost=pl.CostEstimate(flops=PACK_FLOPS, bytes_accessed=PACK_BYTES, transcendentals=0),
+        (opened, tokens, expert_ids, gate_weights, doc_ids),
+        cost=pl.CostEstimate(flops=10**5, bytes_accessed=10**5, transcendentals=0),
     )
     score_full = lax.all_gather(w_score, "tensor", axis=0, tiled=True) if parts > 1 else w_score
     units = w_gate.shape[1]

time: 25.9 us -> 25.3 us (0.977)
  Pallas kernels: 3.18 us -> 2.46 us
    pallas_call x5 -> x6, Pallas kernels: 3.18 us -> 2.46 us  [call(): pl.pallas_call(body, out_shape=tuple(outs), in_specs=[pl.BlockSpec(memory...]
  transfers between devices with their start and end apart: 4 -> 4, of which waited for: 0 -> 0; matrix products, arithmetic and copies ran while one was open for 0% -> 0% of each run, Pallas kernels for 9% -> 7%
where the time goes in v6:
time: 25.3 us; the launch traced here: 25 us
  blocking collectives  20.6 us (81%)
  Pallas kernels  2.46 us (10%)
  between operations  0.74 us (3%)
  starting transfers between devices  0.72 us (3%)
  local copies, waits for them, and re-layouts  0.47 us (2%)
    all_to_all x1, blocking collectives, local(): near = exchange(outgoing, axis_index_groups=first_groups)  11.2 us
    all_to_all x1, blocking collectives, local(): returned = exchange(sending, axis_index_groups=second_groups)  9.4 us
    pallas_call x6, Pallas kernels, call(): pl.pallas_call(body, out_shape=tuple(outs), in_specs=[pl.BlockSpec(memory...  2.46 us
    ppermute x3, starting transfers between devices, local(): other = [lax.ppermute(w, 'expert', swap) for w in (w_gate, w_up, w_down)]  0.65 us
  transfers between devices with their start and end apart: 4, of which 0 were waited for; matrix products, arithmetic and copies ran while one was open for 0% of the time, Pallas kernels for 7%

profile of v6, /device:TPU:1, one launch (start us, length us, event | category | flops | bytes accessed | tf_op | source)
XLA Modules:
  0.0 25.0 jit_solution(10409948833750428420)
XLA Ops:
  0.6 0.0 copy-start.7
  0.6 0.0 copy-start.6
  0.7 0.0 copy-start.5
  0.7 0.0 copy-start.4
  0.7 0.1 collective-permute-start
  0.8 0.5 %collective-permute-start.1 = (bf16[4096,128]{1,0:T(8,128)(2,1)}, bf16[4096,128]{1,0:T(8,128)(2,1)S(1)}, u32[]{:S(2)}, u32[]{:S(2)}) collective-permute-start(bf16[4096,128]{1,0:T(8,128)(2,1)} %refs_2_.1), channel_id=1, source_target_pairs={{0,1},{1,0},{2,3},{3,2},{4,5},{5,4},{6,7},{7,6},{8,9},{9,8},{10,11... | collective-permute-start | bytes 3145736 | tf_op jit(solution)/shard_map/ppermute | solution.py:219
  1.2 0.1 collective-permute-start.2
  1.3 0.0 copy-start
  1.3 0.0 copy-start.1
  1.3 0.0 copy-done.7
  1.3 0.0 copy-done.6
  1.3 0.0 copy-done.5
  1.4 0.0 copy-done.4
  1.4 0.1 shard_map.96
  1.5 11.2 %all_to_all.10.x_ref = bf16[8,2,4224]{2,1,0:T(2,128)(2,1)S(1)} all-to-all(bf16[8,2,4224]{2,1,0:T(2,128)(2,1)S(1)} %shard_map.96), channel_id=1, replica_groups={{11,0,2,4,6,9,13,15},{10,1,3,5,7,8,12,14},{27,16,18,20,22,25,29,31},{26..., dimensions={0} | all-to-all | bytes 270336 | tf_op jit(solution)/shard_map/all_to_all | solution.py:220
  12.7 0.0 copy-start.2
  12.7 0.0 collective-permute-done.refs_1_
  12.7 0.0 collective-permute-done.1.refs_3_
  12.7 0.0 copy-done
  12.7 0.0 copy-done.1
  12.7 0.0 copy-start.3
  12.7 0.7 %shard_map.97 = (bf16[16,256]{1,0:T(8,128)(2,1)S(1)}, f32[16,128]{1,0:T(8,128)S(1)}, f32[8,256]{1,0:T(8,128)S(1)}) custom-call(bf16[8,2,4224]{2,1,0:T(2,128)(2,1)S(1)} %all_to_all.10.x_ref, bf16[4096,128]{1,0:T(8,128)(2,1)S(1)} %copy-done, bf16[4096,128]{1,0:T(8,128)(2,1)S(1)} %collective-permute-done.refs_1_, bf16[4096,128]{1,0:T(8,128)(2,1)S(1)} %copy-done.1, ...), custom_call_target="tpu_custom_call" | custom-call | flops 33554432 | bytes 6291456 | tf_op jit(solution)/shard_map/pallas_call | solution.py:27
  13.4 0.1 collective-permute-start.3
  13.5 0.0 collective-permute-done.2.other_ref
  13.5 0.4 %copy-done.2 = bf16[128,4096]{1,0:T(8,128)(2,1)S(1)} copy-done((bf16[128,4096]{1,0:T(8,128)(2,1)S(1)}, bf16[128,4096]{1,0:T(8,128)(2,1)}, u32[]{:S(2)}) %copy-start.2) | copy-done | bytes 1048600
  13.9 0.0 copy-done.3
  13.9 0.9 %shard_map.98 = (bf16[16,4096]{1,0:T(8,128)(2,1)S(1)}, f32[1,256]{1,0:T(1,128)S(1)}) custom-call(bf16[16,256]{1,0:T(8,128)(2,1)S(1)} %get-tuple-element.9.hidden_ref, f32[16,128]{1,0:T(8,128)S(1)} %get-tuple-element.10.weight_ref, bf16[128,4096]{1,0:T(8,128)(2,1)S(1)} %copy-done.2, bf16[128,4096]{1,0:T(8,128)(2,1)S(1)} %collective-permute-done.2.other_ref, ...), custom_call_target="tpu_custom_call" | custom-call | flops 33554432 | bytes 6291456 | tf_op jit(solution)/shard_map/pallas_call | solution.py:27
  14.8 0.0 collective-permute-done.3.came_ref
  14.8 0.1 shard_map.99
  15.0 9.4 %all_to_all.11.came_ref = bf16[8,2,4224]{2,1,0:T(2,128)(2,1)S(1)} all-to-all(bf16[8,2,4224]{2,1,0:T(2,128)(2,1)S(1)} %get-tuple-element.14), channel_id=1, replica_groups={{11,0,2,4,6,9,13,15},{8,1,3,5,7,10,12,14},{27,16,18,20,22,25,29,31},{24..., dimensions={0} | all-to-all | bytes 270336 | tf_op jit(solution)/shard_map/all_to_all | solution.py:251
  24.4 0.6 %shard_map.100 = (bf16[2,4096]{1,0:T(2,128)(2,1)}, f32[4]{0:T(128)}) custom-call(bf16[8,2,4224]{2,1,0:T(2,128)(2,1)S(1)} %all_to_all.11.came_ref, f32[2,128]{1,0:T(2,128)S(1)} %get-tuple-element.15.stat_ref), custom_call_target="tpu_custom_call" | custom-call | tf_op jit(solution)/shard_map/pallas_call | solution.py:27
  (1 shorter events, 0.0 us)
Async XLA Ops:
  0.6 0.7 %copy-start.7 = (s32[2]{0:T(128)S(1)}, s32[2]{0:T(128)}, u32[]{:S(2)}) copy-start(s32[2]{0:T(128)} %docs_ref.1) | copy-start | bytes 28
  0.6 0.7 %copy-start.6 = (f32[2,2]{1,0:T(2,128)S(1)}, f32[2,2]{1,0:T(2,128)}, u32[]{:S(2)}) copy-start(f32[2,2]{1,0:T(2,128)} %gates_ref.1) | copy-start | bytes 52
  0.7 0.7 %copy-start.5 = (s32[2,2]{1,0:T(2,128)S(1)}, s32[2,2]{1,0:T(2,128)}, u32[]{:S(2)}) copy-start(s32[2,2]{1,0:T(2,128)} %ids_ref.1) | copy-start | bytes 52
  0.7 0.7 %copy-start.4 = (bf16[2,4096]{1,0:T(2,128)(2,1)S(1)}, bf16[2,4096]{1,0:T(2,128)(2,1)}, u32[]{:S(2)}) copy-start(bf16[2,4096]{1,0:T(2,128)(2,1)} %tokens_ref.1) | copy-start | bytes 49156
  0.7 12.0 %collective-permute-start = (bf16[4096,128]{1,0:T(8,128)(2,1)}, bf16[4096,128]{1,0:T(8,128)(2,1)S(1)}, u32[]{:S(2)}, u32[]{:S(2)}) collective-permute-start(bf16[4096,128]{1,0:T(8,128)(2,1)} %refs_0_.1), channel_id=1, source_target_pairs={{0,1},{1,0},{2,3},{3,2},{4,5},{5,4},{6,7},{7,6},{8,9},{9,8},{10,11... | collective-permute-start | bytes 3145736 | tf_op jit(solution)/shard_map/ppermute | solution.py:219
  0.8 12.0 %collective-permute-start.1 = (bf16[4096,128]{1,0:T(8,128)(2,1)}, bf16[4096,128]{1,0:T(8,128)(2,1)S(1)}, u32[]{:S(2)}, u32[]{:S(2)}) collective-permute-start(bf16[4096,128]{1,0:T(8,128)(2,1)} %refs_2_.1), channel_id=1, source_target_pairs={{0,1},{1,0},{2,3},{3,2},{4,5},{5,4},{6,7},{7,6},{8,9},{9,8},{10,11... | collective-permute-start | bytes 3145736 | tf_op jit(solution)/shard_map/ppermute | solution.py:219
  1.2 12.3 %collective-permute-start.2 = (bf16[128,4096]{1,0:T(8,128)(2,1)}, bf16[128,4096]{1,0:T(8,128)(2,1)S(1)}, u32[]{:S(2)}, u32[]{:S(2)}) collective-permute-start(bf16[128,4096]{1,0:T(8,128)(2,1)} %own_ref.1), channel_id=1, source_target_pairs={{0,1},{1,0},{2,3},{3,2},{4,5},{5,4},{6,7},{7,6},{8,9},{9,8},{10,11... | collective-permute-start | bytes 3145736 | tf_op jit(solution)/shard_map/ppermute | solution.py:219
  1.3 11.4 %copy-start = (bf16[4096,128]{1,0:T(8,128)(2,1)S(1)}, bf16[4096,128]{1,0:T(8,128)(2,1)}, u32[]{:S(2)}) copy-start(bf16[4096,128]{1,0:T(8,128)(2,1)} %refs_0_.1) | copy-start | bytes 3145732
  1.3 11.4 %copy-start.1 = (bf16[4096,128]{1,0:T(8,128)(2,1)S(1)}, bf16[4096,128]{1,0:T(8,128)(2,1)}, u32[]{:S(2)}) copy-start(bf16[4096,128]{1,0:T(8,128)(2,1)} %refs_2_.1) | copy-start | bytes 3145732
  12.7 1.2 %copy-start.2 = (bf16[128,4096]{1,0:T(8,128)(2,1)S(1)}, bf16[128,4096]{1,0:T(8,128)(2,1)}, u32[]{:S(2)}) copy-start(bf16[128,4096]{1,0:T(8,128)(2,1)} %own_ref.1) | copy-start | bytes 3145732
  12.7 1.2 %copy-start.3 = (f32[4096]{0:T(1024)S(1)}, f32[4096]{0:T(1024)}, u32[]{:S(2)}) copy-start(f32[4096]{0:T(1024)} %param.15) | copy-start | bytes 49156
  13.4 1.4 %collective-permute-start.3 = (f32[8,256]{1,0:T(8,128)S(1)}, f32[8,256]{1,0:T(8,128)S(1)}, u32[]{:S(2)}, u32[]{:S(2)}) collective-permute-start(f32[8,256]{1,0:T(8,128)S(1)} %get-tuple-element.13.stat_ref), channel_id=1, source_target_pairs={{0,1},{1,0},{2,3},{3,2},{4,5},{5,4},{6,7},{7,6},{8,9},{9,8},{10,11... | collective-permute-start | bytes 24584 | tf_op jit(solution)/shard_map/ppermute | solution.py:236

commit v7 on v6

--- a/solution.py
+++ b/solution.py
@@ -9,6 +9,7 @@
 
 EXP_FLIGHT = 4
 LANES = 128
+DOWN_STEPS = 8
 VMEM_LIMIT = 24 * 1024 * 1024
 OPEN_FLOPS = 10**10
 OPEN_BYTES = 3 * 10**7
@@ -126,13 +127,28 @@
 
 
 def down_body(hidden_ref, weight_ref, own_ref, other_ref, score_ref, out_ref, reach_ref):
-    units = own_ref.shape[0]
-    part = jnp.dot(hidden_ref[:, :units], own_ref[...], preferred_element_type=jnp.float32)
-    part += jnp.dot(hidden_ref[:, units:], other_ref[...], preferred_element_type=jnp.float32)
-    out_ref[...] = (part * weight_ref[:, 0:1]).astype(jnp.bfloat16)
-    score = score_ref[...]
-    reach_ref[:, :units] = score_rows(own_ref[...], score)
-    reach_ref[:, units:] = score_rows(other_ref[...], score)
+    units, width = own_ref.shape
+    step = width // DOWN_STEPS
+    weight = weight_ref[:, 0:1]
+    grown = [jnp.zeros((units, LANES), jnp.float32) for _ in range(2)]
+    for first in range(0, width, step):
+        span = pl.ds(first, step)
+        part = jnp.zeros((hidden_ref.shape[0], step), jnp.float32)
+        for i, ref in enumerate((own_ref, other_ref)):
+            block = ref[:, span]
+            part += jnp.dot(
+                hidden_ref[:, i * units : (i + 1) * units], block, preferred_element_type=jnp.float32
+            )
+            for lane in range(0, step, LANES):
+                tile = block[:, lane : lane + LANES].astype(jnp.float32)
+                grown[i] += tile * score_ref[:, pl.ds(first + lane, LANES)]
+        out_ref[:, span] = (part * weight).astype(jnp.bfloat16)
+    for i in range(2):
+        column = jnp.sum(grown[i], axis=1, keepdims=True)
+        row = lax.broadcasted_iota(jnp.int32, (units, units), 0)
+        lane = lax.broadcasted_iota(jnp.int32, (units, units), 1)
+        turned = jnp.sum(jnp.where(row == lane, column, 0.0), axis=0, keepdims=True)
+        reach_ref[:, i * units : (i + 1) * units] = turned
 
 
 def side_rows(sums, rows):

time: 25.3 us -> 25.1 us (level)
  transfers between devices with their start and end apart: 4 -> 4, of which waited for: 0 -> 0; matrix products, arithmetic and copies ran while one was open for 0% -> 0% of each run, Pallas kernels for 7% -> 6%
where the time goes in v7:
time: 25.1 us; the launch traced here: 24.9 us
  blocking collectives  20.6 us (82%)
  Pallas kernels  2.29 us (9%)
  between operations  0.74 us (3%)
  starting transfers between devices  0.72 us (3%)
  local copies, waits for them, and re-layouts  0.47 us (2%)
    all_to_all x1, blocking collectives, local(): near = exchange(outgoing, axis_index_groups=first_groups)  11.2 us
    all_to_all x1, blocking collectives, local(): returned = exchange(sending, axis_index_groups=second_groups)  9.4 us
    pallas_call x6, Pallas kernels, call(): pl.pallas_call(body, out_shape=tuple(outs), in_specs=[pl.BlockSpec(memory...  2.29 us
    ppermute x3, starting transfers between devices, local(): other = [lax.ppermute(w, 'expert', swap) for w in (w_gate, w_up, w_down)]  0.65 us
  transfers between devices with their start and end apart: 4, of which 0 were waited for; matrix products, arithmetic and copies ran while one was open for 0% of the time, Pallas kernels for 6%

profile of v7, /device:TPU:1, one launch (start us, length us, event | category | flops | bytes accessed | tf_op | source)
XLA Modules:
  0.0 24.9 jit_solution(6831240597150322296)
XLA Ops:
  0.6 0.0 copy-start.7
  0.6 0.0 copy-start.6
  0.7 0.0 copy-start.5
  0.7 0.0 copy-start.4
  0.7 0.1 collective-permute-start
  0.8 0.5 %collective-permute-start.1 = (bf16[4096,128]{1,0:T(8,128)(2,1)}, bf16[4096,128]{1,0:T(8,128)(2,1)S(1)}, u32[]{:S(2)}, u32[]{:S(2)}) collective-permute-start(bf16[4096,128]{1,0:T(8,128)(2,1)} %refs_2_.1), channel_id=1, source_target_pairs={{0,1},{1,0},{2,3},{3,2},{4,5},{5,4},{6,7},{7,6},{8,9},{9,8},{10,11... | collective-permute-start | bytes 3145736 | tf_op jit(solution)/shard_map/ppermute | solution.py:235
  1.2 0.1 collective-permute-start.2
  1.3 0.0 copy-start
  1.3 0.0 copy-start.1
  1.3 0.0 copy-done.7
  1.3 0.0 copy-done.6
  1.3 0.0 copy-done.5
  1.4 0.0 copy-done.4
  1.4 0.1 shard_map.96
  1.5 11.2 %all_to_all.10.x_ref = bf16[8,2,4224]{2,1,0:T(2,128)(2,1)S(1)} all-to-all(bf16[8,2,4224]{2,1,0:T(2,128)(2,1)S(1)} %shard_map.96), channel_id=1, replica_groups={{11,0,2,4,6,9,13,15},{10,1,3,5,7,8,12,14},{27,16,18,20,22,25,29,31},{26..., dimensions={0} | all-to-all | bytes 270336 | tf_op jit(solution)/shard_map/all_to_all | solution.py:236
  12.7 0.0 copy-start.2
  12.7 0.0 collective-permute-done.refs_1_
  12.7 0.0 collective-permute-done.1.refs_3_
  12.7 0.0 copy-done
  12.7 0.0 copy-done.1
  12.7 0.0 copy-start.3
  12.7 0.7 %shard_map.97 = (bf16[16,256]{1,0:T(8,128)(2,1)S(1)}, f32[16,128]{1,0:T(8,128)S(1)}, f32[8,256]{1,0:T(8,128)S(1)}) custom-call(bf16[8,2,4224]{2,1,0:T(2,128)(2,1)S(1)} %all_to_all.10.x_ref, bf16[4096,128]{1,0:T(8,128)(2,1)S(1)} %copy-done, bf16[4096,128]{1,0:T(8,128)(2,1)S(1)} %collective-permute-done.refs_1_, bf16[4096,128]{1,0:T(8,128)(2,1)S(1)} %copy-done.1, ...), custom_call_target="tpu_custom_call" | custom-call | flops 33554432 | bytes 6291456 | tf_op jit(solution)/shard_map/pallas_call | solution.py:28
  13.4 0.1 collective-permute-start.3
  13.5 0.0 collective-permute-done.2.other_ref
  13.5 0.4 %copy-done.2 = bf16[128,4096]{1,0:T(8,128)(2,1)S(1)} copy-done((bf16[128,4096]{1,0:T(8,128)(2,1)S(1)}, bf16[128,4096]{1,0:T(8,128)(2,1)}, u32[]{:S(2)}) %copy-start.2) | copy-done | bytes 1048600
  13.9 0.0 copy-done.3
  13.9 0.8 %shard_map.98 = (bf16[16,4096]{1,0:T(8,128)(2,1)S(1)}, f32[1,256]{1,0:T(1,128)S(1)}) custom-call(bf16[16,256]{1,0:T(8,128)(2,1)S(1)} %get-tuple-element.9.hidden_ref, f32[16,128]{1,0:T(8,128)S(1)} %get-tuple-element.10.weight_ref, bf16[128,4096]{1,0:T(8,128)(2,1)S(1)} %copy-done.2, bf16[128,4096]{1,0:T(8,128)(2,1)S(1)} %collective-permute-done.2.other_ref, ...), custom_call_target="tpu_custom_call" | custom-call | flops 33554432 | bytes 6291456 | tf_op jit(solution)/shard_map/pallas_call | solution.py:28
  14.7 0.0 collective-permute-done.3.came_ref
  14.7 0.1 shard_map.99
  14.8 9.4 %all_to_all.11.came_ref = bf16[8,2,4224]{2,1,0:T(2,128)(2,1)S(1)} all-to-all(bf16[8,2,4224]{2,1,0:T(2,128)(2,1)S(1)} %get-tuple-element.14), channel_id=1, replica_groups={{11,0,2,4,6,9,13,15},{8,1,3,5,7,10,12,14},{27,16,18,20,22,25,29,31},{24..., dimensions={0} | all-to-all | bytes 270336 | tf_op jit(solution)/shard_map/all_to_all | solution.py:267
  24.2 0.6 %shard_map.100 = (bf16[2,4096]{1,0:T(2,128)(2,1)}, f32[4]{0:T(128)}) custom-call(bf16[8,2,4224]{2,1,0:T(2,128)(2,1)S(1)} %all_to_all.11.came_ref, f32[2,128]{1,0:T(2,128)S(1)} %get-tuple-element.15.stat_ref), custom_call_target="tpu_custom_call" | custom-call | tf_op jit(solution)/shard_map/pallas_call | solution.py:28
  (1 shorter events, 0.0 us)
Async XLA Ops:
  0.6 0.7 %copy-start.7 = (s32[2]{0:T(128)S(1)}, s32[2]{0:T(128)}, u32[]{:S(2)}) copy-start(s32[2]{0:T(128)} %docs_ref.1) | copy-start | bytes 28
  0.6 0.7 %copy-start.6 = (f32[2,2]{1,0:T(2,128)S(1)}, f32[2,2]{1,0:T(2,128)}, u32[]{:S(2)}) copy-start(f32[2,2]{1,0:T(2,128)} %gates_ref.1) | copy-start | bytes 52
  0.7 0.7 %copy-start.5 = (s32[2,2]{1,0:T(2,128)S(1)}, s32[2,2]{1,0:T(2,128)}, u32[]{:S(2)}) copy-start(s32[2,2]{1,0:T(2,128)} %ids_ref.1) | copy-start | bytes 52
  0.7 0.7 %copy-start.4 = (bf16[2,4096]{1,0:T(2,128)(2,1)S(1)}, bf16[2,4096]{1,0:T(2,128)(2,1)}, u32[]{:S(2)}) copy-start(bf16[2,4096]{1,0:T(2,128)(2,1)} %tokens_ref.1) | copy-start | bytes 49156
  0.7 12.0 %collective-permute-start = (bf16[4096,128]{1,0:T(8,128)(2,1)}, bf16[4096,128]{1,0:T(8,128)(2,1)S(1)}, u32[]{:S(2)}, u32[]{:S(2)}) collective-permute-start(bf16[4096,128]{1,0:T(8,128)(2,1)} %refs_0_.1), channel_id=1, source_target_pairs={{0,1},{1,0},{2,3},{3,2},{4,5},{5,4},{6,7},{7,6},{8,9},{9,8},{10,11... | collective-permute-start | bytes 3145736 | tf_op jit(solution)/shard_map/ppermute | solution.py:235
  0.8 12.0 %collective-permute-start.1 = (bf16[4096,128]{1,0:T(8,128)(2,1)}, bf16[4096,128]{1,0:T(8,128)(2,1)S(1)}, u32[]{:S(2)}, u32[]{:S(2)}) collective-permute-start(bf16[4096,128]{1,0:T(8,128)(2,1)} %refs_2_.1), channel_id=1, source_target_pairs={{0,1},{1,0},{2,3},{3,2},{4,5},{5,4},{6,7},{7,6},{8,9},{9,8},{10,11... | collective-permute-start | bytes 3145736 | tf_op jit(solution)/shard_map/ppermute | solution.py:235
  1.2 12.3 %collective-permute-start.2 = (bf16[128,4096]{1,0:T(8,128)(2,1)}, bf16[128,4096]{1,0:T(8,128)(2,1)S(1)}, u32[]{:S(2)}, u32[]{:S(2)}) collective-permute-start(bf16[128,4096]{1,0:T(8,128)(2,1)} %own_ref.1), channel_id=1, source_target_pairs={{0,1},{1,0},{2,3},{3,2},{4,5},{5,4},{6,7},{7,6},{8,9},{9,8},{10,11... | collective-permute-start | bytes 3145736 | tf_op jit(solution)/shard_map/ppermute | solution.py:235
  1.3 11.4 %copy-start = (bf16[4096,128]{1,0:T(8,128)(2,1)S(1)}, bf16[4096,128]{1,0:T(8,128)(2,1)}, u32[]{:S(2)}) copy-start(bf16[4096,128]{1,0:T(8,128)(2,1)} %refs_0_.1) | copy-start | bytes 3145732
  1.3 11.4 %copy-start.1 = (bf16[4096,128]{1,0:T(8,128)(2,1)S(1)}, bf16[4096,128]{1,0:T(8,128)(2,1)}, u32[]{:S(2)}) copy-start(bf16[4096,128]{1,0:T(8,128)(2,1)} %refs_2_.1) | copy-start | bytes 3145732
  12.7 1.2 %copy-start.2 = (bf16[128,4096]{1,0:T(8,128)(2,1)S(1)}, bf16[128,4096]{1,0:T(8,128)(2,1)}, u32[]{:S(2)}) copy-start(bf16[128,4096]{1,0:T(8,128)(2,1)} %own_ref.1) | copy-start | bytes 3145732
  12.7 1.2 %copy-start.3 = (f32[4096]{0:T(1024)S(1)}, f32[4096]{0:T(1024)}, u32[]{:S(2)}) copy-start(f32[4096]{0:T(1024)} %param.15) | copy-start | bytes 49156
  13.4 1.3 %collective-permute-start.3 = (f32[8,256]{1,0:T(8,128)S(1)}, f32[8,256]{1,0:T(8,128)S(1)}, u32[]{:S(2)}, u32[]{:S(2)}) collective-permute-start(f32[8,256]{1,0:T(8,128)S(1)} %get-tuple-element.13.stat_ref), channel_id=1, source_target_pairs={{0,1},{1,0},{2,3},{3,2},{4,5},{5,4},{6,7},{7,6},{8,9},{9,8},{10,11... | collective-permute-start | bytes 24584 | tf_op jit(solution)/shard_map/ppermute | solution.py:252

commit v8 on v7

--- a/solution.py
+++ b/solution.py
@@ -37,12 +37,13 @@
 
 
 def exchange_groups(half):
-    middle = half // 2
+    middle, last = half // 2, half - half // 4
+    ends = [0, *range(last, half), *range(1, last)]
     exchanges = []
     for roots in ((middle + 1, middle + 1), (middle + 1, middle)):
         groups = []
         for side, root in enumerate(roots):
-            order = [root] + [q for q in range(half) if q != root]
+            order = [root] + [q for q in ends if q != root]
             groups.append([2 * q + (int(q >= middle) ^ side) for q in order])
         exchanges.append(groups)
     return exchanges
@@ -78,26 +79,6 @@
         out_ref[b, :, width:] = side
 
 
-def hidden_rows(held, w_gate, w_up):
-    gate = jnp.dot(held, w_gate, preferred_element_type=jnp.float32)
-    up = jnp.dot(held, w_up, preferred_element_type=jnp.float32)
-    return (gate / (1.0 + jnp.exp(-gate)) * up).astype(jnp.bfloat16)
-
-
-def score_rows(w_down, score):
-    row = lax.broadcasted_iota(jnp.int32, (8, score.shape[1]), 0)
-    pieces = jnp.zeros((8, score.shape[1]), jnp.float32)
-    rest = score
-    for i in range(3):
-        piece = rest.astype(jnp.bfloat16).astype(jnp.float32)
-        pieces = jnp.where(row == i, piece, pieces)
-        rest = rest - piece
-    added = lax.dot_general(
-        pieces.astype(jnp.bfloat16), w_down, (((1,), (1,)), ((), ())), preferred_element_type=jnp.float32
-    )
-    return jnp.sum(added, axis=0, keepdims=True)
-
-
 def hidden_body(spread, doc_total, x_ref, *refs):
     gates, ups = refs[0:2], refs[2:4]
     hidden_ref, weight_ref, stat_ref = refs[4:]
@@ -117,8 +98,11 @@
     hits = jnp.where(doc == lane.astype(jnp.float32), 1.0, 0.0)
     stat_ref[doc_total : doc_total + 1, :LANES] = jnp.sum(hits, axis=0, keepdims=True)
     units = gates[0].shape[1]
+    wide = [jnp.concatenate([gates[i][...], ups[i][...]], axis=1) for i in range(2)]
+    both = [jnp.dot(held, w, preferred_element_type=jnp.float32) for w in wide]
     for i in range(2):
-        hidden = hidden_rows(held, gates[i][...], ups[i][...])
+        gate, up = both[i][:, :units], both[i][:, units:]
+        hidden = (gate / (1.0 + jnp.exp(-gate)) * up).astype(jnp.bfloat16)
         hidden_ref[:, i * units : (i + 1) * units] = hidden
         hidden = hidden.astype(jnp.float32) * weight
         for d in range(doc_total):

time: 25.1 us -> 24.7 us (0.984)
  blocking collectives: 20.6 us -> 20.2 us
where the time goes in v8:
time: 24.7 us; the launch traced here: 24.5 us
  blocking collectives  20.2 us (82%)
  Pallas kernels  2.3 us (9%)
  between operations  0.74 us (3%)
  starting transfers between devices  0.72 us (3%)
  local copies, waits for them, and re-layouts  0.46 us (2%)
    all_to_all x1, blocking collectives, local(): near = exchange(outgoing, axis_index_groups=first_groups)  11 us
    all_to_all x1, blocking collectives, local(): returned = exchange(sending, axis_index_groups=second_groups)  9.17 us
    pallas_call x6, Pallas kernels, call(): pl.pallas_call(body, out_shape=tuple(outs), in_specs=[pl.BlockSpec(memory...  2.3 us
    ppermute x3, starting transfers between devices, local(): other = [lax.ppermute(w, 'expert', swap) for w in (w_gate, w_up, w_down)]  0.65 us
  transfers between devices with their start and end apart: 4, of which 0 were waited for; matrix products, arithmetic and copies ran while one was open for 0% of the time, Pallas kernels for 6%

profile of v8, /device:TPU:1, one launch (start us, length us, event | category | flops | bytes accessed | tf_op | source)
XLA Modules:
  0.0 24.5 jit_solution(5276951484963299714)
XLA Ops:
  0.6 0.0 copy-start.7
  0.6 0.0 copy-start.6
  0.7 0.0 copy-start.5
  0.7 0.0 copy-start.4
  0.7 0.1 collective-permute-start
  0.8 0.5 %collective-permute-start.1 = (bf16[4096,128]{1,0:T(8,128)(2,1)}, bf16[4096,128]{1,0:T(8,128)(2,1)S(1)}, u32[]{:S(2)}, u32[]{:S(2)}) collective-permute-start(bf16[4096,128]{1,0:T(8,128)(2,1)} %refs_2_.1), channel_id=1, source_target_pairs={{0,1},{1,0},{2,3},{3,2},{4,5},{5,4},{6,7},{7,6},{8,9},{9,8},{10,11... | collective-permute-start | bytes 3145736 | tf_op jit(solution)/shard_map/ppermute | solution.py:219
  1.2 0.1 collective-permute-start.2
  1.3 0.0 copy-start
  1.3 0.0 copy-start.1
  1.3 0.0 copy-done.7
  1.3 0.0 copy-done.6
  1.3 0.0 copy-done.5
  1.4 0.0 copy-done.4
  1.4 0.1 shard_map.96
  1.5 11.0 %all_to_all.10.x_ref = bf16[8,2,4224]{2,1,0:T(2,128)(2,1)S(1)} all-to-all(bf16[8,2,4224]{2,1,0:T(2,128)(2,1)S(1)} %shard_map.96), channel_id=1, replica_groups={{11,0,13,15,2,4,6,9},{10,1,12,14,3,5,7,8},{27,16,29,31,18,20,22,25},{26..., dimensions={0} | all-to-all | bytes 270336 | tf_op jit(solution)/shard_map/all_to_all | solution.py:220
  12.5 0.0 copy-start.2
  12.5 0.0 collective-permute-done.refs_1_
  12.5 0.0 collective-permute-done.1.refs_3_
  12.5 0.0 copy-done
  12.5 0.0 copy-done.1
  12.6 0.0 copy-start.3
  12.6 0.7 %shard_map.97 = (bf16[16,256]{1,0:T(8,128)(2,1)S(1)}, f32[16,128]{1,0:T(8,128)S(1)}, f32[8,256]{1,0:T(8,128)S(1)}) custom-call(bf16[8,2,4224]{2,1,0:T(2,128)(2,1)S(1)} %all_to_all.10.x_ref, bf16[4096,128]{1,0:T(8,128)(2,1)S(1)} %copy-done, bf16[4096,128]{1,0:T(8,128)(2,1)S(1)} %collective-permute-done.refs_1_, bf16[4096,128]{1,0:T(8,128)(2,1)S(1)} %copy-done.1, ...), custom_call_target="tpu_custom_call" | custom-call | flops 33554432 | bytes 6291456 | tf_op jit(solution)/shard_map/pallas_call | solution.py:28
  13.3 0.1 collective-permute-start.3
  13.3 0.0 collective-permute-done.2.other_ref
  13.4 0.4 %copy-done.2 = bf16[128,4096]{1,0:T(8,128)(2,1)S(1)} copy-done((bf16[128,4096]{1,0:T(8,128)(2,1)S(1)}, bf16[128,4096]{1,0:T(8,128)(2,1)}, u32[]{:S(2)}) %copy-start.2) | copy-done | bytes 1048600
  13.8 0.0 copy-done.3
  13.8 0.8 %shard_map.98 = (bf16[16,4096]{1,0:T(8,128)(2,1)S(1)}, f32[1,256]{1,0:T(1,128)S(1)}) custom-call(bf16[16,256]{1,0:T(8,128)(2,1)S(1)} %get-tuple-element.9.hidden_ref, f32[16,128]{1,0:T(8,128)S(1)} %get-tuple-element.10.weight_ref, bf16[128,4096]{1,0:T(8,128)(2,1)S(1)} %copy-done.2, bf16[128,4096]{1,0:T(8,128)(2,1)S(1)} %collective-permute-done.2.other_ref, ...), custom_call_target="tpu_custom_call" | custom-call | flops 33554432 | bytes 6291456 | tf_op jit(solution)/shard_map/pallas_call | solution.py:28
  14.5 0.0 collective-permute-done.3.came_ref
  14.5 0.1 shard_map.99
  14.6 9.2 %all_to_all.11.came_ref = bf16[8,2,4224]{2,1,0:T(2,128)(2,1)S(1)} all-to-all(bf16[8,2,4224]{2,1,0:T(2,128)(2,1)S(1)} %get-tuple-element.14), channel_id=1, replica_groups={{11,0,13,15,2,4,6,9},{8,1,12,14,3,5,7,10},{27,16,29,31,18,20,22,25},{24..., dimensions={0} | all-to-all | bytes 270336 | tf_op jit(solution)/shard_map/all_to_all | solution.py:251
  23.8 0.6 %shard_map.100 = (bf16[2,4096]{1,0:T(2,128)(2,1)}, f32[4]{0:T(128)}) custom-call(bf16[8,2,4224]{2,1,0:T(2,128)(2,1)S(1)} %all_to_all.11.came_ref, f32[2,128]{1,0:T(2,128)S(1)} %get-tuple-element.15.stat_ref), custom_call_target="tpu_custom_call" | custom-call | tf_op jit(solution)/shard_map/pallas_call | solution.py:28
  (1 shorter events, 0.0 us)
Async XLA Ops:
  0.6 0.7 %copy-start.7 = (s32[2]{0:T(128)S(1)}, s32[2]{0:T(128)}, u32[]{:S(2)}) copy-start(s32[2]{0:T(128)} %docs_ref.1) | copy-start | bytes 28
  0.6 0.7 %copy-start.6 = (f32[2,2]{1,0:T(2,128)S(1)}, f32[2,2]{1,0:T(2,128)}, u32[]{:S(2)}) copy-start(f32[2,2]{1,0:T(2,128)} %gates_ref.1) | copy-start | bytes 52
  0.7 0.7 %copy-start.5 = (s32[2,2]{1,0:T(2,128)S(1)}, s32[2,2]{1,0:T(2,128)}, u32[]{:S(2)}) copy-start(s32[2,2]{1,0:T(2,128)} %ids_ref.1) | copy-start | bytes 52
  0.7 0.7 %copy-start.4 = (bf16[2,4096]{1,0:T(2,128)(2,1)S(1)}, bf16[2,4096]{1,0:T(2,128)(2,1)}, u32[]{:S(2)}) copy-start(bf16[2,4096]{1,0:T(2,128)(2,1)} %tokens_ref.1) | copy-start | bytes 49156
  0.7 11.9 %collective-permute-start = (bf16[4096,128]{1,0:T(8,128)(2,1)}, bf16[4096,128]{1,0:T(8,128)(2,1)S(1)}, u32[]{:S(2)}, u32[]{:S(2)}) collective-permute-start(bf16[4096,128]{1,0:T(8,128)(2,1)} %refs_0_.1), channel_id=1, source_target_pairs={{0,1},{1,0},{2,3},{3,2},{4,5},{5,4},{6,7},{7,6},{8,9},{9,8},{10,11... | collective-permute-start | bytes 3145736 | tf_op jit(solution)/shard_map/ppermute | solution.py:219
  0.8 11.8 %collective-permute-start.1 = (bf16[4096,128]{1,0:T(8,128)(2,1)}, bf16[4096,128]{1,0:T(8,128)(2,1)S(1)}, u32[]{:S(2)}, u32[]{:S(2)}) collective-permute-start(bf16[4096,128]{1,0:T(8,128)(2,1)} %refs_2_.1), channel_id=1, source_target_pairs={{0,1},{1,0},{2,3},{3,2},{4,5},{5,4},{6,7},{7,6},{8,9},{9,8},{10,11... | collective-permute-start | bytes 3145736 | tf_op jit(solution)/shard_map/ppermute | solution.py:219
  1.2 12.1 %collective-permute-start.2 = (bf16[128,4096]{1,0:T(8,128)(2,1)}, bf16[128,4096]{1,0:T(8,128)(2,1)S(1)}, u32[]{:S(2)}, u32[]{:S(2)}) collective-permute-start(bf16[128,4096]{1,0:T(8,128)(2,1)} %own_ref.1), channel_id=1, source_target_pairs={{0,1},{1,0},{2,3},{3,2},{4,5},{5,4},{6,7},{7,6},{8,9},{9,8},{10,11... | collective-permute-start | bytes 3145736 | tf_op jit(solution)/shard_map/ppermute | solution.py:219
  1.3 11.2 %copy-start = (bf16[4096,128]{1,0:T(8,128)(2,1)S(1)}, bf16[4096,128]{1,0:T(8,128)(2,1)}, u32[]{:S(2)}) copy-start(bf16[4096,128]{1,0:T(8,128)(2,1)} %refs_0_.1) | copy-start | bytes 3145732
  1.3 11.2 %copy-start.1 = (bf16[4096,128]{1,0:T(8,128)(2,1)S(1)}, bf16[4096,128]{1,0:T(8,128)(2,1)}, u32[]{:S(2)}) copy-start(bf16[4096,128]{1,0:T(8,128)(2,1)} %refs_2_.1) | copy-start | bytes 3145732
  12.5 1.2 %copy-start.2 = (bf16[128,4096]{1,0:T(8,128)(2,1)S(1)}, bf16[128,4096]{1,0:T(8,128)(2,1)}, u32[]{:S(2)}) copy-start(bf16[128,4096]{1,0:T(8,128)(2,1)} %own_ref.1) | copy-start | bytes 3145732
  12.6 1.2 %copy-start.3 = (f32[4096]{0:T(1024)S(1)}, f32[4096]{0:T(1024)}, u32[]{:S(2)}) copy-start(f32[4096]{0:T(1024)} %param.15) | copy-start | bytes 49156
  13.3 1.2 %collective-permute-start.3 = (f32[8,256]{1,0:T(8,128)S(1)}, f32[8,256]{1,0:T(8,128)S(1)}, u32[]{:S(2)}, u32[]{:S(2)}) collective-permute-start(f32[8,256]{1,0:T(8,128)S(1)} %get-tuple-element.13.stat_ref), channel_id=1, source_target_pairs={{0,1},{1,0},{2,3},{3,2},{4,5},{5,4},{6,7},{7,6},{8,9},{9,8},{10,11... | collective-permute-start | bytes 24584 | tf_op jit(solution)/shard_map/ppermute | solution.py:236

commit v9 on v8

--- a/solution.py
+++ b/solution.py
@@ -38,9 +38,11 @@
 
 def exchange_groups(half):
     middle, last = half // 2, half - half // 4
-    ends = [0, *range(last, half), *range(1, last)]
+    inner = list(range(1, last))
+    far = list(range(last, half))
+    rows = ([0, *far, *inner], [0, *reversed(far), *inner])
     exchanges = []
-    for roots in ((middle + 1, middle + 1), (middle + 1, middle)):
+    for ends, roots in zip(rows, ((middle + 1, middle + 1), (middle + 1, middle))):
         groups = []
         for side, root in enumerate(roots):
             order = [root] + [q for q in ends if q != root]

time: 24.7 us -> 24.7 us (level)
  no operation moved by 1% of the time
where the time goes in v9:
time: 24.7 us; the launch traced here: 24.4 us
  blocking collectives  20.2 us (82%)
  Pallas kernels  2.3 us (9%)
  between operations  0.74 us (3%)
  starting transfers between devices  0.72 us (3%)
  local copies, waits for them, and re-layouts  0.46 us (2%)
    all_to_all x1, blocking collectives, local(): near = exchange(outgoing, axis_index_groups=first_groups)  11 us
    all_to_all x1, blocking collectives, local(): returned = exchange(sending, axis_index_groups=second_groups)  9.15 us
    pallas_call x6, Pallas kernels, call(): pl.pallas_call(body, out_shape=tuple(outs), in_specs=[pl.BlockSpec(memory...  2.3 us
    ppermute x3, starting transfers between devices, local(): other = [lax.ppermute(w, 'expert', swap) for w in (w_gate, w_up, w_down)]  0.65 us
  transfers between devices with their start and end apart: 4, of which 0 were waited for; matrix products, arithmetic and copies ran while one was open for 0% of the time, Pallas kernels for 6%

profile of v9, /device:TPU:1, one launch (start us, length us, event | category | flops | bytes accessed | tf_op | source)
XLA Modules:
  0.0 24.4 jit_solution(3335821316367478019)
XLA Ops:
  0.6 0.0 copy-start.7
  0.6 0.0 copy-start.6
  0.7 0.0 copy-start.5
  0.7 0.0 copy-start.4
  0.7 0.1 collective-permute-start
  0.8 0.5 %collective-permute-start.1 = (bf16[4096,128]{1,0:T(8,128)(2,1)}, bf16[4096,128]{1,0:T(8,128)(2,1)S(1)}, u32[]{:S(2)}, u32[]{:S(2)}) collective-permute-start(bf16[4096,128]{1,0:T(8,128)(2,1)} %refs_2_.1), channel_id=1, source_target_pairs={{0,1},{1,0},{2,3},{3,2},{4,5},{5,4},{6,7},{7,6},{8,9},{9,8},{10,11... | collective-permute-start | bytes 3145736 | tf_op jit(solution)/shard_map/ppermute | solution.py:221
  1.2 0.1 collective-permute-start.2
  1.3 0.0 copy-start
  1.3 0.0 copy-start.1
  1.3 0.0 copy-done.7
  1.3 0.0 copy-done.6
  1.3 0.0 copy-done.5
  1.4 0.0 copy-done.4
  1.4 0.1 shard_map.96
  1.5 11.0 %all_to_all.10.x_ref = bf16[8,2,4224]{2,1,0:T(2,128)(2,1)S(1)} all-to-all(bf16[8,2,4224]{2,1,0:T(2,128)(2,1)S(1)} %shard_map.96), channel_id=1, replica_groups={{11,0,13,15,2,4,6,9},{10,1,12,14,3,5,7,8},{27,16,29,31,18,20,22,25},{26..., dimensions={0} | all-to-all | bytes 270336 | tf_op jit(solution)/shard_map/all_to_all | solution.py:222
  12.5 0.0 copy-start.2
  12.5 0.0 collective-permute-done.refs_1_
  12.5 0.0 collective-permute-done.1.refs_3_
  12.5 0.0 copy-done
  12.5 0.0 copy-done.1
  12.6 0.0 copy-start.3
  12.6 0.7 %shard_map.97 = (bf16[16,256]{1,0:T(8,128)(2,1)S(1)}, f32[16,128]{1,0:T(8,128)S(1)}, f32[8,256]{1,0:T(8,128)S(1)}) custom-call(bf16[8,2,4224]{2,1,0:T(2,128)(2,1)S(1)} %all_to_all.10.x_ref, bf16[4096,128]{1,0:T(8,128)(2,1)S(1)} %copy-done, bf16[4096,128]{1,0:T(8,128)(2,1)S(1)} %collective-permute-done.refs_1_, bf16[4096,128]{1,0:T(8,128)(2,1)S(1)} %copy-done.1, ...), custom_call_target="tpu_custom_call" | custom-call | flops 33554432 | bytes 6291456 | tf_op jit(solution)/shard_map/pallas_call | solution.py:28
  13.3 0.1 collective-permute-start.3
  13.3 0.0 collective-permute-done.2.other_ref
  13.4 0.4 %copy-done.2 = bf16[128,4096]{1,0:T(8,128)(2,1)S(1)} copy-done((bf16[128,4096]{1,0:T(8,128)(2,1)S(1)}, bf16[128,4096]{1,0:T(8,128)(2,1)}, u32[]{:S(2)}) %copy-start.2) | copy-done | bytes 1048600
  13.8 0.0 copy-done.3
  13.8 0.8 %shard_map.98 = (bf16[16,4096]{1,0:T(8,128)(2,1)S(1)}, f32[1,256]{1,0:T(1,128)S(1)}) custom-call(bf16[16,256]{1,0:T(8,128)(2,1)S(1)} %get-tuple-element.9.hidden_ref, f32[16,128]{1,0:T(8,128)S(1)} %get-tuple-element.10.weight_ref, bf16[128,4096]{1,0:T(8,128)(2,1)S(1)} %copy-done.2, bf16[128,4096]{1,0:T(8,128)(2,1)S(1)} %collective-permute-done.2.other_ref, ...), custom_call_target="tpu_custom_call" | custom-call | flops 33554432 | bytes 6291456 | tf_op jit(solution)/shard_map/pallas_call | solution.py:28
  14.5 0.0 collective-permute-done.3.came_ref
  14.5 0.1 shard_map.99
  14.6 9.2 %all_to_all.11.came_ref = bf16[8,2,4224]{2,1,0:T(2,128)(2,1)S(1)} all-to-all(bf16[8,2,4224]{2,1,0:T(2,128)(2,1)S(1)} %get-tuple-element.14), channel_id=1, replica_groups={{11,0,15,13,2,4,6,9},{8,1,14,12,3,5,7,10},{27,16,31,29,18,20,22,25},{24..., dimensions={0} | all-to-all | bytes 270336 | tf_op jit(solution)/shard_map/all_to_all | solution.py:253
  23.8 0.6 %shard_map.100 = (bf16[2,4096]{1,0:T(2,128)(2,1)}, f32[4]{0:T(128)}) custom-call(bf16[8,2,4224]{2,1,0:T(2,128)(2,1)S(1)} %all_to_all.11.came_ref, f32[2,128]{1,0:T(2,128)S(1)} %get-tuple-element.15.stat_ref), custom_call_target="tpu_custom_call" | custom-call | tf_op jit(solution)/shard_map/pallas_call | solution.py:28
  (1 shorter events, 0.0 us)
Async XLA Ops:
  0.6 0.7 %copy-start.7 = (s32[2]{0:T(128)S(1)}, s32[2]{0:T(128)}, u32[]{:S(2)}) copy-start(s32[2]{0:T(128)} %docs_ref.1) | copy-start | bytes 28
  0.6 0.7 %copy-start.6 = (f32[2,2]{1,0:T(2,128)S(1)}, f32[2,2]{1,0:T(2,128)}, u32[]{:S(2)}) copy-start(f32[2,2]{1,0:T(2,128)} %gates_ref.1) | copy-start | bytes 52
  0.7 0.7 %copy-start.5 = (s32[2,2]{1,0:T(2,128)S(1)}, s32[2,2]{1,0:T(2,128)}, u32[]{:S(2)}) copy-start(s32[2,2]{1,0:T(2,128)} %ids_ref.1) | copy-start | bytes 52
  0.7 0.7 %copy-start.4 = (bf16[2,4096]{1,0:T(2,128)(2,1)S(1)}, bf16[2,4096]{1,0:T(2,128)(2,1)}, u32[]{:S(2)}) copy-start(bf16[2,4096]{1,0:T(2,128)(2,1)} %tokens_ref.1) | copy-start | bytes 49156
  0.7 11.9 %collective-permute-start = (bf16[4096,128]{1,0:T(8,128)(2,1)}, bf16[4096,128]{1,0:T(8,128)(2,1)S(1)}, u32[]{:S(2)}, u32[]{:S(2)}) collective-permute-start(bf16[4096,128]{1,0:T(8,128)(2,1)} %refs_0_.1), channel_id=1, source_target_pairs={{0,1},{1,0},{2,3},{3,2},{4,5},{5,4},{6,7},{7,6},{8,9},{9,8},{10,11... | collective-permute-start | bytes 3145736 | tf_op jit(solution)/shard_map/ppermute | solution.py:221
  0.8 11.8 %collective-permute-start.1 = (bf16[4096,128]{1,0:T(8,128)(2,1)}, bf16[4096,128]{1,0:T(8,128)(2,1)S(1)}, u32[]{:S(2)}, u32[]{:S(2)}) collective-permute-start(bf16[4096,128]{1,0:T(8,128)(2,1)} %refs_2_.1), channel_id=1, source_target_pairs={{0,1},{1,0},{2,3},{3,2},{4,5},{5,4},{6,7},{7,6},{8,9},{9,8},{10,11... | collective-permute-start | bytes 3145736 | tf_op jit(solution)/shard_map/ppermute | solution.py:221
  1.2 12.1 %collective-permute-start.2 = (bf16[128,4096]{1,0:T(8,128)(2,1)}, bf16[128,4096]{1,0:T(8,128)(2,1)S(1)}, u32[]{:S(2)}, u32[]{:S(2)}) collective-permute-start(bf16[128,4096]{1,0:T(8,128)(2,1)} %own_ref.1), channel_id=1, source_target_pairs={{0,1},{1,0},{2,3},{3,2},{4,5},{5,4},{6,7},{7,6},{8,9},{9,8},{10,11... | collective-permute-start | bytes 3145736 | tf_op jit(solution)/shard_map/ppermute | solution.py:221
  1.3 11.2 %copy-start = (bf16[4096,128]{1,0:T(8,128)(2,1)S(1)}, bf16[4096,128]{1,0:T(8,128)(2,1)}, u32[]{:S(2)}) copy-start(bf16[4096,128]{1,0:T(8,128)(2,1)} %refs_0_.1) | copy-start | bytes 3145732
  1.3 11.2 %copy-start.1 = (bf16[4096,128]{1,0:T(8,128)(2,1)S(1)}, bf16[4096,128]{1,0:T(8,128)(2,1)}, u32[]{:S(2)}) copy-start(bf16[4096,128]{1,0:T(8,128)(2,1)} %refs_2_.1) | copy-start | bytes 3145732
  12.5 1.2 %copy-start.2 = (bf16[128,4096]{1,0:T(8,128)(2,1)S(1)}, bf16[128,4096]{1,0:T(8,128)(2,1)}, u32[]{:S(2)}) copy-start(bf16[128,4096]{1,0:T(8,128)(2,1)} %own_ref.1) | copy-start | bytes 3145732
  12.6 1.2 %copy-start.3 = (f32[4096]{0:T(1024)S(1)}, f32[4096]{0:T(1024)}, u32[]{:S(2)}) copy-start(f32[4096]{0:T(1024)} %param.15) | copy-start | bytes 49156
  13.3 1.2 %collective-permute-start.3 = (f32[8,256]{1,0:T(8,128)S(1)}, f32[8,256]{1,0:T(8,128)S(1)}, u32[]{:S(2)}, u32[]{:S(2)}) collective-permute-start(f32[8,256]{1,0:T(8,128)S(1)} %get-tuple-element.13.stat_ref), channel_id=1, source_target_pairs={{0,1},{1,0},{2,3},{3,2},{4,5},{5,4},{6,7},{7,6},{8,9},{9,8},{10,11... | collective-permute-start | bytes 24584 | tf_op jit(solution)/shard_map/ppermute | solution.py:238
